TPU v7x, 32 devices: a whole 2x2x4 slice. The times are simulated.
32 devices in a mesh: data: 8 (over z, y), pipe: 4 (over x, core).
Axes of the slice: x: 2, y: 2, z: 4, core: 2. Of those that a mesh axis runs over, the one named last changes fastest.
Arguments:
- acts_in: bfloat16 [192, 64, 512], P(('data', 'pipe'))
- cot_out: bfloat16 [192, 64, 512], P(('data', 'pipe'))
- seq_lens: int32 [192], P(('data', 'pipe'))
- w_qkv: bfloat16 [4, 512, 1536], P('pipe')
- w_out: bfloat16 [4, 8, 64, 512], P('pipe')
- w_up: bfloat16 [4, 512, 2048], P('pipe')
- w_down: bfloat16 [4, 2048, 512], P('pipe')
- gain_attn: bfloat16 [4, 512], P('pipe')
- gain_mlp: bfloat16 [4, 512], P('pipe')
Outputs:
- output 1: bfloat16 [192, 64, 512], P(('data', 'pipe'))
- output 2: float32 [4, 512, 1536], P('pipe')
- output 3: float32 [4, 8, 64, 512], P('pipe')
- output 4: float32 [4, 512, 2048], P('pipe')
- output 5: float32 [4, 2048, 512], P('pipe')
- output 6: float32 [4, 512], P('pipe')
- output 7: float32 [4, 512], P('pipe')
All inputs are finite; a program needn't handle non-finite values.
Results may differ from a plain program's by a relative error of at most 0.02.
Values are sent between devices in bfloat16 or wider.
A program may use at most 1 GiB of HBM per device.

v0:
```python
import functools
import jax
import jax.numpy as jnp
from jax import lax
from jax.sharding import PartitionSpec as P, NamedSharding

NORM_EPS = 1e-5


def norm_f32(hid_f32, gain_f32):
    inv_rms = lax.rsqrt(jnp.mean(hid_f32 * hid_f32, axis=-1, keepdims=True) + NORM_EPS)
    return hid_f32 * inv_rms * gain_f32


def attention_core(q_heads, k_heads, v_heads, visible):
    scale = q_heads.shape[-1] ** -0.5
    scores = jnp.einsum('mqhe,mkhe->mhqk', q_heads, k_heads, preferred_element_type=jnp.float32) * scale
    scores = jnp.where(visible[:, None], scores, -1e30)
    attn_probs = jax.nn.softmax(scores, axis=-1).astype(jnp.bfloat16)
    return jnp.einsum('mhqk,mkhe->mqhe', attn_probs, v_heads, preferred_element_type=jnp.float32).astype(jnp.bfloat16)


def layer_forward(hidden, layer_w, visible):
    w_qkv, w_out, w_up, w_down, gain_attn, gain_mlp = layer_w
    n_micro, seq_size = hidden.shape[0], hidden.shape[1]
    heads, head_dim = w_out.shape[0], w_out.shape[1]
    hid_f32 = hidden.astype(jnp.float32)
    normed_a = norm_f32(hid_f32, gain_attn.astype(jnp.float32)).astype(jnp.bfloat16)
    qkv_all = jnp.einsum('msd,de->mse', normed_a, w_qkv, preferred_element_type=jnp.float32)
    qkv_all = qkv_all.astype(jnp.bfloat16).reshape(n_micro, seq_size, 3, heads, head_dim)
    context = attention_core(qkv_all[:, :, 0], qkv_all[:, :, 1], qkv_all[:, :, 2], visible)
    attn_out = jnp.einsum('mshe,hed->msd', context, w_out, preferred_element_type=jnp.float32)
    mid_hidden = (hid_f32 + attn_out).astype(jnp.bfloat16)
    mid_up = mid_hidden.astype(jnp.float32)
    normed_m = norm_f32(mid_up, gain_mlp.astype(jnp.float32)).astype(jnp.bfloat16)
    pre_act = jnp.einsum('msd,df->msf', normed_m, w_up, preferred_element_type=jnp.float32)
    gelu_out = jax.nn.gelu(pre_act, approximate=False).astype(jnp.bfloat16)
    mlp_out = jnp.einsum('msf,fd->msd', gelu_out, w_down, preferred_element_type=jnp.float32)
    out_hidden = (mid_up + mlp_out).astype(jnp.bfloat16)
    saved = (hidden, normed_a, qkv_all, context, mid_hidden, normed_m, pre_act, gelu_out)
    return out_hidden, saved


def layer_backward(d_hidden, saved, layer_w, visible):
    w_qkv, w_out, w_up, w_down, gain_attn, gain_mlp = layer_w
    hidden, normed_a, qkv_all, context, mid_hidden, normed_m, pre_act, gelu_out = saved
    n_micro, seq_size = hidden.shape[0], hidden.shape[1]
    d_top = d_hidden.astype(jnp.bfloat16)
    grad_down = jnp.einsum('msf,msd->fd', gelu_out, d_top, preferred_element_type=jnp.float32)
    d_gelu = jnp.einsum('msd,fd->msf', d_top, w_down, preferred_element_type=jnp.float32)
    gelu_pull = jax.vjp(functools.partial(jax.nn.gelu, approximate=False), pre_act)[1]
    d_pre = gelu_pull(d_gelu)[0].astype(jnp.bfloat16)
    grad_up = jnp.einsum('msd,msf->df', normed_m, d_pre, preferred_element_type=jnp.float32)
    d_normed_m = jnp.einsum('msf,df->msd', d_pre, w_up, preferred_element_type=jnp.float32)
    norm_pull_m = jax.vjp(norm_f32, mid_hidden.astype(jnp.float32), gain_mlp.astype(jnp.float32))[1]
    d_mid_norm, grad_gain_mlp = norm_pull_m(d_normed_m)
    d_mid = d_hidden + d_mid_norm
    d_mid_bf = d_mid.astype(jnp.bfloat16)
    grad_out = jnp.einsum('mshe,msd->hed', context, d_mid_bf, preferred_element_type=jnp.float32)
    d_context = jnp.einsum('msd,hed->mshe', d_mid_bf, w_out, preferred_element_type=jnp.float32).astype(jnp.bfloat16)
    attn_pull = jax.vjp(lambda q_in, k_in, v_in: attention_core(q_in, k_in, v_in, visible), qkv_all[:, :, 0], qkv_all[:, :, 1], qkv_all[:, :, 2])[1]
    d_query, d_key, d_value = attn_pull(d_context)
    d_qkv = jnp.stack([d_query, d_key, d_value], axis=2).reshape(n_micro, seq_size, -1)
    grad_qkv = jnp.einsum('msd,mse->de', normed_a, d_qkv, preferred_element_type=jnp.float32)
    d_normed_a = jnp.einsum('mse,de->msd', d_qkv, w_qkv, preferred_element_type=jnp.float32)
    norm_pull_a = jax.vjp(norm_f32, hidden.astype(jnp.float32), gain_attn.astype(jnp.float32))[1]
    d_in_norm, grad_gain_attn = norm_pull_a(d_normed_a)
    return d_mid + d_in_norm, (grad_qkv, grad_out, grad_up, grad_down, grad_gain_attn, grad_gain_mlp)


def stage_forward(hidden, stage_w, visible):
    for layer_idx in range(stage_w[0].shape[0]):
        hidden = layer_forward(hidden, tuple(w_part[layer_idx] for w_part in stage_w), visible)[0]
    return hidden


def stage_backward(stage_in, d_hidden, stage_w, visible):
    num_local = stage_w[0].shape[0]
    saved_all = []
    hidden = stage_in
    for layer_idx in range(num_local):
        hidden, saved_acts = layer_forward(hidden, tuple(w_part[layer_idx] for w_part in stage_w), visible)
        saved_all.append(saved_acts)
    grads_rev = []
    for layer_idx in reversed(range(num_local)):
        d_hidden, layer_grads = layer_backward(d_hidden, saved_all[layer_idx], tuple(w_part[layer_idx] for w_part in stage_w), visible)
        grads_rev.append(layer_grads)
    grads_by_layer = grads_rev[::-1]
    stage_grads = tuple(jnp.stack([layer_grads[part_idx] for layer_grads in grads_by_layer]) for part_idx in range(6))
    return d_hidden, stage_grads


def solution(mesh):
    row_spec = P(('data', 'pipe'))
    stage_spec = P('pipe')
    pipe_size = mesh.shape['pipe']
    num_slots = 2 * pipe_size - 1
    fwd_perm = [(src_dev, (src_dev - 1) % pipe_size) for src_dev in range(pipe_size)]
    bwd_perm = [(src_dev, (src_dev + 1) % pipe_size) for src_dev in range(pipe_size)]
    home_shift = 2 % pipe_size
    home_perm = [(src_dev, (src_dev + home_shift) % pipe_size) for src_dev in range(pipe_size)]

    def device_pass(acts_in, cot_out, seq_lens, w_qkv, w_out, w_up, w_down, gain_attn, gain_mlp):
        own_w = (w_qkv, w_out, w_up, w_down, gain_attn, gain_mlp)
        pipe_pos = lax.axis_index('pipe')
        fwd_offset = (pipe_size - pipe_pos) % pipe_size
        bwd_offset = (pipe_pos + 1) % pipe_size
        positions = jnp.arange(acts_in.shape[1])
        causal = positions[None, None, :] <= positions[None, :, None]
        visible = causal & (positions[None, None, :] < seq_lens[:, None, None])
        valid = (positions[None, :] < seq_lens[:, None])[:, :, None]

        def fwd_slot(slot, hidden, stage_inputs, held_w):
            slot_rel = slot - fwd_offset
            active = (slot_rel >= 0) & (slot_rel < pipe_size)
            stage_idx = jnp.clip(slot_rel, 0, pipe_size - 1)

            def run_stage(operands):
                hid_state, inputs_buf = operands
                inputs_buf = lax.dynamic_update_index_in_dim(inputs_buf, hid_state, stage_idx, 0)
                return stage_forward(hid_state, held_w, visible), inputs_buf

            return lax.cond(active, run_stage, lambda operands: operands, (hidden, stage_inputs))

        def fwd_body(slot, loop_carry):
            hidden, stage_inputs, held_w = loop_carry
            held_w = tuple(lax.ppermute(w_part, 'pipe', fwd_perm) for w_part in held_w)
            hidden, stage_inputs = fwd_slot(slot, hidden, stage_inputs, held_w)
            return hidden, stage_inputs, held_w

        stage_inputs = jnp.zeros((pipe_size,) + acts_in.shape, acts_in.dtype)
        hidden, stage_inputs = fwd_slot(0, acts_in, stage_inputs, own_w)
        hidden, stage_inputs, _ = lax.fori_loop(1, num_slots, fwd_body, (hidden, stage_inputs, own_w))
        acts_out = jnp.where(valid, hidden, jnp.zeros_like(hidden))

        def bwd_slot(slot, d_hidden, held_w, held_acc):
            slot_rel = slot - bwd_offset
            active = (slot_rel >= 0) & (slot_rel < pipe_size)
            stage_idx = pipe_size - 1 - jnp.clip(slot_rel, 0, pipe_size - 1)

            def run_stage(operands):
                d_state, acc_in = operands
                stage_in = lax.dynamic_index_in_dim(stage_inputs, stage_idx, 0, keepdims=False)
                d_new, stage_grads = stage_backward(stage_in, d_state, held_w, visible)
                return d_new, tuple(acc_part + grad_part for acc_part, grad_part in zip(acc_in, stage_grads))

            return lax.cond(active, run_stage, lambda operands: operands, (d_hidden, held_acc))

        def bwd_body(slot, loop_carry):
            d_hidden, held_w, held_acc = loop_carry
            held_w = tuple(lax.ppermute(w_part, 'pipe', bwd_perm) for w_part in held_w)
            held_acc = tuple(lax.ppermute(acc_part, 'pipe', bwd_perm) for acc_part in held_acc)
            d_hidden, held_acc = bwd_slot(slot, d_hidden, held_w, held_acc)
            return d_hidden, held_w, held_acc

        d_hidden = jnp.where(valid, cot_out.astype(jnp.float32), 0.0)
        zero_acc = tuple(jnp.zeros(w_part.shape, jnp.float32) for w_part in own_w)
        d_hidden, held_acc = bwd_slot(0, d_hidden, own_w, zero_acc)
        _, _, held_acc = lax.fori_loop(1, num_slots, bwd_body, (d_hidden, own_w, held_acc))
        if home_shift:
            held_acc = tuple(lax.ppermute(acc_part, 'pipe', home_perm) for acc_part in held_acc)
        grads = tuple(lax.psum(acc_part, 'data') for acc_part in held_acc)
        return (acts_out,) + grads

    return jax.shard_map(device_pass, mesh=mesh, in_specs=(row_spec, row_spec, row_spec) + (stage_spec,) * 6, out_specs=(row_spec,) + (stage_spec,) * 6, check_vma=False)
```

profile of v0, /device:TPU:0, one launch (start us, length us, event | category | flops | bytes accessed | tf_op | source)
XLA Modules:
  0.0 3238.9 jit_solution(8743636150485073851)
XLA Ops:
  23.0 29.0 conditional.4
  52.0 616.9 %while.66 = (s32[]{:T(128)}, bf16[6,64,512]{2,1,0:T(8,128)(2,1)S(1)}, bf16[4,6,64,512]{3,2,1,0:T(8,128)(2,1)S(1)}, bf16[1,512,1536]{2,1,0:T(8,128)(2,1)}, bf16[1...) while((s32[]{:T(128)}, ...), condition=%wide.region_13.14_spmd.clone, body=%wide.region_6.13_spmd.clone.sunk | while | flops 2536993792 | bytes 85058216 | solution.py:133
  54.6 66.2 %collective-permute-done = bf16[1,512]{1,0:T(2,128)(2,1)S(1)} collective-permute-done((bf16[1,512]{1,0:T(2,128)(2,1)S(1)}, bf16[1,512]{1,0:T(2,128)(2,1)S(1)}, u32[]{:S(2)}, u32[]{:S(2)}) %collective-permute-start) | collective-permute-done | bytes 1056 | tf_op jit(solution)/shard_map/while/body/eval_jaxpr/ppermute | solution.py:127
  128.1 23.9 conditional.10
  143.1 8.9 fusion.113
  162.2 66.2 %collective-permute-done = bf16[1,512]{1,0:T(2,128)(2,1)S(1)} collective-permute-done((bf16[1,512]{1,0:T(2,128)(2,1)S(1)}, bf16[1,512]{1,0:T(2,128)(2,1)S(1)}, u32[]{:S(2)}, u32[]{:S(2)}) %collective-permute-start) | collective-permute-done | bytes 1056 | tf_op jit(solution)/shard_map/while/body/eval_jaxpr/ppermute | solution.py:127
  235.8 23.9 conditional.10
  250.8 8.9 fusion.113
  269.9 66.2 %collective-permute-done = bf16[1,512]{1,0:T(2,128)(2,1)S(1)} collective-permute-done((bf16[1,512]{1,0:T(2,128)(2,1)S(1)}, bf16[1,512]{1,0:T(2,128)(2,1)S(1)}, u32[]{:S(2)}, u32[]{:S(2)}) %collective-permute-start) | collective-permute-done | bytes 1056 | tf_op jit(solution)/shard_map/while/body/eval_jaxpr/ppermute | solution.py:127
  343.5 23.9 conditional.10
  377.6 66.2 %collective-permute-done = bf16[1,512]{1,0:T(2,128)(2,1)S(1)} collective-permute-done((bf16[1,512]{1,0:T(2,128)(2,1)S(1)}, bf16[1,512]{1,0:T(2,128)(2,1)S(1)}, u32[]{:S(2)}, u32[]{:S(2)}) %collective-permute-start) | collective-permute-done | bytes 1056 | tf_op jit(solution)/shard_map/while/body/eval_jaxpr/ppermute | solution.py:127
  457.4 25.6 collective-permute-start.4
  485.2 66.2 %collective-permute-done = bf16[1,512]{1,0:T(2,128)(2,1)S(1)} collective-permute-done((bf16[1,512]{1,0:T(2,128)(2,1)S(1)}, bf16[1,512]{1,0:T(2,128)(2,1)S(1)}, u32[]{:S(2)}, u32[]{:S(2)}) %collective-permute-start) | collective-permute-done | bytes 1056 | tf_op jit(solution)/shard_map/while/body/eval_jaxpr/ppermute | solution.py:127
  566.8 22.1 collective-permute-start.5
  589.0 46.2 %collective-permute-done = bf16[1,512]{1,0:T(2,128)(2,1)S(1)} collective-permute-done((bf16[1,512]{1,0:T(2,128)(2,1)S(1)}, bf16[1,512]{1,0:T(2,128)(2,1)S(1)}, u32[]{:S(2)}, u32[]{:S(2)}) %collective-permute-start) | collective-permute-done | bytes 1056 | tf_op jit(solution)/shard_map/while/body/eval_jaxpr/ppermute | solution.py:127
  637.8 20.4 collective-permute-done.3
  669.6 23.1 conditional.5
  696.0 1853.6 %while.67 = (s32[]{:T(128)}, f32[6,64,512]{2,1,0:T(8,128)}, bf16[1,512,1536]{2,1,0:T(8,128)(2,1)}, bf16[1,8,64,512]{3,2,1,0:T(8,128)(2,1)}, bf16[1,512,2048]{2,1...) while((s32[]{:T(128)}, f32[6,64,512]{2,1,0:T(8,128)}, ...), condition=%wide.region_37.38_spmd.clone, body=%wide.region_25.37_spmd.clone.sunk | while | flops 6692323328 | bytes 326480192 | solution.py:159
  696.0 26.3 collective-permute-start.8
  722.3 28.8 collective-permute-start.13
  751.2 113.0 %collective-permute-done.12 = bf16[1,512]{1,0:T(2,128)(2,1)S(1)} collective-permute-done((bf16[1,512]{1,0:T(2,128)(2,1)}, bf16[1,512]{1,0:T(2,128)(2,1)S(1)}, u32[]{:S(2)}, u32[]{:S(2)}) %collective-permute-start.12) | collective-permute-done | bytes 1056 | tf_op jit(solution)/shard_map/while/body/eval_jaxpr/ppermute | solution.py:151
  871.0 24.6 collective-permute-done.16
  895.7 56.2 %collective-permute-done.17 = bf16[1,2048,512]{2,1,0:T(8,128)(2,1)} collective-permute-done((bf16[1,2048,512]{2,1,0:T(8,128)(2,1)}, bf16[1,2048,512]{2,1,0:T(8,128)(2,1)}, u32[]{:S(2)}, u32[]{:S(2)}) %collective-permute-start.17) | collective-permute-done | bytes 2097184 | tf_op jit(solution)/shard_map/while/body/eval_jaxpr/ppermute | solution.py:151
  963.9 84.3 %conditional.11 = ((f32[6,64,512]{2,1,0:T(8,128)}, f32[1,512,1536]{2,1,0:T(8,128)S(1)}, f32[1,8,64,512]{3,2,1,0:T(8,128)}, f32[1,512,2048]{2,1,0:T(8,128)}, f32[...) conditional(s32[]{:T(128)} %convert_element_type.719, (f32[6,64,512]{2,1,0:T(8,128)}, ...), branch_computations={%region_26.26_spmd, %region_27.0_spmd} | conditional | flops 6692323328 | bytes 198514528 | solution.py:147
  1065.8 113.0 %collective-permute-done.12 = bf16[1,512]{1,0:T(2,128)(2,1)S(1)} collective-permute-done((bf16[1,512]{1,0:T(2,128)(2,1)}, bf16[1,512]{1,0:T(2,128)(2,1)S(1)}, u32[]{:S(2)}, u32[]{:S(2)}) %collective-permute-start.12) | collective-permute-done | bytes 1056 | tf_op jit(solution)/shard_map/while/body/eval_jaxpr/ppermute | solution.py:151
  1185.7 24.6 collective-permute-done.16
  1210.3 56.2 %collective-permute-done.17 = bf16[1,2048,512]{2,1,0:T(8,128)(2,1)} collective-permute-done((bf16[1,2048,512]{2,1,0:T(8,128)(2,1)}, bf16[1,2048,512]{2,1,0:T(8,128)(2,1)}, u32[]{:S(2)}, u32[]{:S(2)}) %collective-permute-start.17) | collective-permute-done | bytes 2097184 | tf_op jit(solution)/shard_map/while/body/eval_jaxpr/ppermute | solution.py:151
  1278.6 84.3 %conditional.11 = ((f32[6,64,512]{2,1,0:T(8,128)}, f32[1,512,1536]{2,1,0:T(8,128)S(1)}, f32[1,8,64,512]{3,2,1,0:T(8,128)}, f32[1,512,2048]{2,1,0:T(8,128)}, f32[...) conditional(s32[]{:T(128)} %convert_element_type.719, (f32[6,64,512]{2,1,0:T(8,128)}, ...), branch_computations={%region_26.26_spmd, %region_27.0_spmd} | conditional | flops 6692323328 | bytes 198514528 | solution.py:147
  1380.5 113.0 %collective-permute-done.12 = bf16[1,512]{1,0:T(2,128)(2,1)S(1)} collective-permute-done((bf16[1,512]{1,0:T(2,128)(2,1)}, bf16[1,512]{1,0:T(2,128)(2,1)S(1)}, u32[]{:S(2)}, u32[]{:S(2)}) %collective-permute-start.12) | collective-permute-done | bytes 1056 | tf_op jit(solution)/shard_map/while/body/eval_jaxpr/ppermute | solution.py:151
  1500.3 24.6 collective-permute-done.16
  1525.0 56.2 %collective-permute-done.17 = bf16[1,2048,512]{2,1,0:T(8,128)(2,1)} collective-permute-done((bf16[1,2048,512]{2,1,0:T(8,128)(2,1)}, bf16[1,2048,512]{2,1,0:T(8,128)(2,1)}, u32[]{:S(2)}, u32[]{:S(2)}) %collective-permute-start.17) | collective-permute-done | bytes 2097184 | tf_op jit(solution)/shard_map/while/body/eval_jaxpr/ppermute | solution.py:151
  1593.2 84.3 %conditional.11 = ((f32[6,64,512]{2,1,0:T(8,128)}, f32[1,512,1536]{2,1,0:T(8,128)S(1)}, f32[1,8,64,512]{3,2,1,0:T(8,128)}, f32[1,512,2048]{2,1,0:T(8,128)}, f32[...) conditional(s32[]{:T(128)} %convert_element_type.719, (f32[6,64,512]{2,1,0:T(8,128)}, ...), branch_computations={%region_26.26_spmd, %region_27.0_spmd} | conditional | flops 6692323328 | bytes 198514528 | solution.py:147
  1695.1 113.0 %collective-permute-done.12 = bf16[1,512]{1,0:T(2,128)(2,1)S(1)} collective-permute-done((bf16[1,512]{1,0:T(2,128)(2,1)}, bf16[1,512]{1,0:T(2,128)(2,1)S(1)}, u32[]{:S(2)}, u32[]{:S(2)}) %collective-permute-start.12) | collective-permute-done | bytes 1056 | tf_op jit(solution)/shard_map/while/body/eval_jaxpr/ppermute | solution.py:151
  1814.9 24.6 collective-permute-done.16
  1839.6 56.2 %collective-permute-done.17 = bf16[1,2048,512]{2,1,0:T(8,128)(2,1)} collective-permute-done((bf16[1,2048,512]{2,1,0:T(8,128)(2,1)}, bf16[1,2048,512]{2,1,0:T(8,128)(2,1)}, u32[]{:S(2)}, u32[]{:S(2)}) %collective-permute-start.17) | collective-permute-done | bytes 2097184 | tf_op jit(solution)/shard_map/while/body/eval_jaxpr/ppermute | solution.py:151
  1907.8 84.3 %conditional.11 = ((f32[6,64,512]{2,1,0:T(8,128)}, f32[1,512,1536]{2,1,0:T(8,128)S(1)}, f32[1,8,64,512]{3,2,1,0:T(8,128)}, f32[1,512,2048]{2,1,0:T(8,128)}, f32[...) conditional(s32[]{:T(128)} %convert_element_type.719, (f32[6,64,512]{2,1,0:T(8,128)}, ...), branch_computations={%region_26.26_spmd, %region_27.0_spmd} | conditional | flops 6692323328 | bytes 198514528 | solution.py:147
  2009.7 113.0 %collective-permute-done.12 = bf16[1,512]{1,0:T(2,128)(2,1)S(1)} collective-permute-done((bf16[1,512]{1,0:T(2,128)(2,1)}, bf16[1,512]{1,0:T(2,128)(2,1)S(1)}, u32[]{:S(2)}, u32[]{:S(2)}) %collective-permute-start.12) | collective-permute-done | bytes 1056 | tf_op jit(solution)/shard_map/while/body/eval_jaxpr/ppermute | solution.py:151
  2129.6 24.6 collective-permute-done.16
  2154.2 56.2 %collective-permute-done.17 = bf16[1,2048,512]{2,1,0:T(8,128)(2,1)} collective-permute-done((bf16[1,2048,512]{2,1,0:T(8,128)(2,1)}, bf16[1,2048,512]{2,1,0:T(8,128)(2,1)}, u32[]{:S(2)}, u32[]{:S(2)}) %collective-permute-start.17) | collective-permute-done | bytes 2097184 | tf_op jit(solution)/shard_map/while/body/eval_jaxpr/ppermute | solution.py:151
  2237.7 84.1 %collective-permute-start.8 = (f32[1,512,2048]{2,1,0:T(8,128)}, f32[1,512,2048]{2,1,0:T(8,128)}, u32[]{:S(2)}, u32[]{:S(2)}) collective-permute-start(f32[1,512,2048]{2,1,0:T(8,128)} %get-tuple-element.1270), channel_id=1, source_target_pairs={{0,1},{1,2},{2,3},{3,0},{4,5},{5,6},{6,7},{7,4},{8,9},{9,10},{10,1... | collective-permute-start | bytes 12582920 | tf_op jit(solution)/shard_map/while/body/eval_jaxpr/ppermute | solution.py:152
  2324.0 68.2 %collective-permute-done.12 = bf16[1,512]{1,0:T(2,128)(2,1)S(1)} collective-permute-done((bf16[1,512]{1,0:T(2,128)(2,1)}, bf16[1,512]{1,0:T(2,128)(2,1)S(1)}, u32[]{:S(2)}, u32[]{:S(2)}) %collective-permute-start.12) | collective-permute-done | bytes 1056 | tf_op jit(solution)/shard_map/while/body/eval_jaxpr/ppermute | solution.py:151
  2392.2 42.4 %collective-permute-start.15 = (bf16[1,512]{1,0:T(2,128)(2,1)}, bf16[1,512]{1,0:T(2,128)(2,1)S(1)}, u32[]{:S(2)}, u32[]{:S(2)}) collective-permute-start(bf16[1,512]{1,0:T(2,128)(2,1)} %get-tuple-element.1267), channel_id=1, source_target_pairs={{0,1},{1,2},{2,3},{3,0},{4,5},{5,6},{6,7},{7,4},{8,9},{9,10},{10,1... | collective-permute-start | bytes 3080 | tf_op jit(solution)/shard_map/while/body/eval_jaxpr/ppermute | solution.py:151
  2444.0 20.6 collective-permute-done.16
  2466.1 54.6 %collective-permute-done.17 = bf16[1,2048,512]{2,1,0:T(8,128)(2,1)} collective-permute-done((bf16[1,2048,512]{2,1,0:T(8,128)(2,1)}, bf16[1,2048,512]{2,1,0:T(8,128)(2,1)}, u32[]{:S(2)}, u32[]{:S(2)}) %collective-permute-start.17) | collective-permute-done | bytes 2097184 | tf_op jit(solution)/shard_map/while/body/eval_jaxpr/ppermute | solution.py:151
  2549.6 86.7 %collective-permute-start.20 = (f32[1,512,2048]{2,1,0:T(8,128)}, f32[1,512,2048]{2,1,0:T(8,128)}, u32[]{:S(2)}, u32[]{:S(2)}) collective-permute-start(f32[1,512,2048]{2,1,0:T(8,128)} %get-tuple-element.747), channel_id=1, source_target_pairs={{0,2},{1,3},{2,0},{3,1},{4,6},{5,7},{6,4},{7,5},{8,10},{9,11},{10,... | collective-permute-start | bytes 12582920 | tf_op jit(solution)/shard_map/ppermute | solution.py:161
  2638.4 186.0 %collective-permute-done.19 = f32[1,8,64,512]{3,2,1,0:T(8,128)S(1)} collective-permute-done((f32[1,8,64,512]{3,2,1,0:T(8,128)}, f32[1,8,64,512]{3,2,1,0:T(8,128)S(1)}, u32[]{:S(2)}, u32[]{:S(2)}) %collective-permute-start.19) | collective-permute-done | bytes 1048608 | tf_op jit(solution)/shard_map/ppermute | solution.py:161
  2831.0 24.1 all-reduce
  2855.1 366.0 %all-reduce.4.cloned.1.call-done = (f32[1,512,1536]{2,1,0:T(8,128)}, f32[1,8,64,512]{3,2,1,0:T(8,128)}, f32[1,512,2048]{2,1,0:T(8,128)}, f32[1,2048,512]{2,1,0:T(8,128)}) async-done(((f32[1,512,1536]{2,1,0:T(8,128)}, f32[1,8,64,512]{3,2,1,0:T(8,128)}, f32[1,512,2048]{2,1,0:T(8,128)}, f32[1,2048,512]{2,1,0:T(8,128)}), (f32[1,512,1536]{2,1,0:T(8,128)}, f32[1,8,64,512]{3,2,1,0:T(8,128)}, ...) | async-done | bytes 12582928 | tf_op jit(solution)/shard_map/psum | solution.py:162
  (947 shorter events, 781.5 us)
Async XLA Ops:
  7.2 3213.9 %all-reduce.4.cloned.1.call-start = ((), (), s32[]{:S(2)}) async-start(), calls=%async_computation | async-start | bytes 25165824 | tf_op jit(solution)/shard_map/psum | solution.py:162
  457.4 101.4 %collective-permute-start.4 = (bf16[1,512,2048]{2,1,0:T(8,128)(2,1)}, bf16[1,512,2048]{2,1,0:T(8,128)(2,1)}, u32[]{:S(2)}, u32[]{:S(2)}) collective-permute-start(bf16[1,512,2048]{2,1,0:T(8,128)(2,1)} %get-tuple-element.1200), channel_id=1, source_target_pairs={{0,3},{1,0},{2,1},{3,2},{4,7},{5,4},{6,5},{7,6},{8,11},{9,8},{10,9... | collective-permute-start | bytes 6291464 | tf_op jit(solution)/shard_map/while/body/eval_jaxpr/ppermute | solution.py:127
  565.1 97.2 %collective-permute-start.4 = (bf16[1,512,2048]{2,1,0:T(8,128)(2,1)}, bf16[1,512,2048]{2,1,0:T(8,128)(2,1)}, u32[]{:S(2)}, u32[]{:S(2)}) collective-permute-start(bf16[1,512,2048]{2,1,0:T(8,128)(2,1)} %get-tuple-element.1200), channel_id=1, source_target_pairs={{0,3},{1,0},{2,1},{3,2},{4,7},{5,4},{6,5},{7,6},{8,11},{9,8},{10,9... | collective-permute-start | bytes 6291464 | tf_op jit(solution)/shard_map/while/body/eval_jaxpr/ppermute | solution.py:127
  566.8 95.5 %collective-permute-start.5 = (bf16[1,2048,512]{2,1,0:T(8,128)(2,1)}, bf16[1,2048,512]{2,1,0:T(8,128)(2,1)}, u32[]{:S(2)}, u32[]{:S(2)}) collective-permute-start(bf16[1,2048,512]{2,1,0:T(8,128)(2,1)} %get-tuple-element.1201), channel_id=1, source_target_pairs={{0,3},{1,0},{2,1},{3,2},{4,7},{5,4},{6,5},{7,6},{8,11},{9,8},{10,9... | collective-permute-start | bytes 6291464 | tf_op jit(solution)/shard_map/while/body/eval_jaxpr/ppermute | solution.py:127
  696.0 267.9 %collective-permute-start.8 = (f32[1,512,2048]{2,1,0:T(8,128)}, f32[1,512,2048]{2,1,0:T(8,128)}, u32[]{:S(2)}, u32[]{:S(2)}) collective-permute-start(f32[1,512,2048]{2,1,0:T(8,128)} %get-tuple-element.1270), channel_id=1, source_target_pairs={{0,1},{1,2},{2,3},{3,0},{4,5},{5,6},{6,7},{7,4},{8,9},{9,10},{10,1... | collective-permute-start | bytes 12582920 | tf_op jit(solution)/shard_map/while/body/eval_jaxpr/ppermute | solution.py:152
  722.3 241.6 %collective-permute-start.9 = (f32[1,2048,512]{2,1,0:T(8,128)}, f32[1,2048,512]{2,1,0:T(8,128)}, u32[]{:S(2)}, u32[]{:S(2)}) collective-permute-start(f32[1,2048,512]{2,1,0:T(8,128)} %get-tuple-element.1271), channel_id=1, source_target_pairs={{0,1},{1,2},{2,3},{3,0},{4,5},{5,6},{6,7},{7,4},{8,9},{9,10},{10,1... | collective-permute-start | bytes 12582920 | tf_op jit(solution)/shard_map/while/body/eval_jaxpr/ppermute | solution.py:152
  722.3 148.8 %collective-permute-start.13 = (bf16[1,512,1536]{2,1,0:T(8,128)(2,1)}, bf16[1,512,1536]{2,1,0:T(8,128)(2,1)}, u32[]{:S(2)}, u32[]{:S(2)}) collective-permute-start(bf16[1,512,1536]{2,1,0:T(8,128)(2,1)} %get-tuple-element.1262), channel_id=1, source_target_pairs={{0,1},{1,2},{2,3},{3,0},{4,5},{5,6},{6,7},{7,4},{8,9},{9,10},{10,1... | collective-permute-start | bytes 4718600 | tf_op jit(solution)/shard_map/while/body/eval_jaxpr/ppermute | solution.py:151
  751.1 119.1 %collective-permute-start.14 = (bf16[1,8,64,512]{3,2,1,0:T(8,128)(2,1)}, bf16[1,8,64,512]{3,2,1,0:T(8,128)(2,1)S(1)}, u32[]{:S(2)}, u32[]{:S(2)}) collective-permute-start(bf16[1,8,64,512]{3,2,1,0:T(8,128)(2,1)} %get-tuple-element.1263), channel_id=1, source_target_pairs={{0,1},{1,2},{2,3},{3,0},{4,5},{5,6},{6,7},{7,4},{8,9},{9,10},{10,1... | collective-permute-start | bytes 1572872 | tf_op jit(solution)/shard_map/while/body/eval_jaxpr/ppermute | solution.py:151
  751.1 113.1 %collective-permute-start.12 = (bf16[1,512]{1,0:T(2,128)(2,1)}, bf16[1,512]{1,0:T(2,128)(2,1)S(1)}, u32[]{:S(2)}, u32[]{:S(2)}) collective-permute-start(bf16[1,512]{1,0:T(2,128)(2,1)} %get-tuple-element.1266), channel_id=1, source_target_pairs={{0,1},{1,2},{2,3},{3,0},{4,5},{5,6},{6,7},{7,4},{8,9},{9,10},{10,1... | collective-permute-start | bytes 3080 | tf_op jit(solution)/shard_map/while/body/eval_jaxpr/ppermute | solution.py:151
  871.0 92.9 %collective-permute-start.6 = (f32[1,512,1536]{2,1,0:T(8,128)}, f32[1,512,1536]{2,1,0:T(8,128)S(1)}, u32[]{:S(2)}, u32[]{:S(2)}) collective-permute-start(f32[1,512,1536]{2,1,0:T(8,128)} %get-tuple-element.1268), channel_id=1, source_target_pairs={{0,1},{1,2},{2,3},{3,0},{4,5},{5,6},{6,7},{7,4},{8,9},{9,10},{10,1... | collective-permute-start | bytes 9437192 | tf_op jit(solution)/shard_map/while/body/eval_jaxpr/ppermute | solution.py:152
  871.0 80.8 %collective-permute-start.17 = (bf16[1,2048,512]{2,1,0:T(8,128)(2,1)}, bf16[1,2048,512]{2,1,0:T(8,128)(2,1)}, u32[]{:S(2)}, u32[]{:S(2)}) collective-permute-start(bf16[1,2048,512]{2,1,0:T(8,128)(2,1)} %get-tuple-element.1265), channel_id=1, source_target_pairs={{0,1},{1,2},{2,3},{3,0},{4,5},{5,6},{6,7},{7,4},{8,9},{9,10},{10,1... | collective-permute-start | bytes 6291464 | tf_op jit(solution)/shard_map/while/body/eval_jaxpr/ppermute | solution.py:151
  1063.5 215.0 %collective-permute-start.8 = (f32[1,512,2048]{2,1,0:T(8,128)}, f32[1,512,2048]{2,1,0:T(8,128)}, u32[]{:S(2)}, u32[]{:S(2)}) collective-permute-start(f32[1,512,2048]{2,1,0:T(8,128)} %get-tuple-element.1270), channel_id=1, source_target_pairs={{0,1},{1,2},{2,3},{3,0},{4,5},{5,6},{6,7},{7,4},{8,9},{9,10},{10,1... | collective-permute-start | bytes 12582920 | tf_op jit(solution)/shard_map/while/body/eval_jaxpr/ppermute | solution.py:152
  1063.5 215.0 %collective-permute-start.9 = (f32[1,2048,512]{2,1,0:T(8,128)}, f32[1,2048,512]{2,1,0:T(8,128)}, u32[]{:S(2)}, u32[]{:S(2)}) collective-permute-start(f32[1,2048,512]{2,1,0:T(8,128)} %get-tuple-element.1271), channel_id=1, source_target_pairs={{0,1},{1,2},{2,3},{3,0},{4,5},{5,6},{6,7},{7,4},{8,9},{9,10},{10,1... | collective-permute-start | bytes 12582920 | tf_op jit(solution)/shard_map/while/body/eval_jaxpr/ppermute | solution.py:152
  1063.6 122.1 %collective-permute-start.13 = (bf16[1,512,1536]{2,1,0:T(8,128)(2,1)}, bf16[1,512,1536]{2,1,0:T(8,128)(2,1)}, u32[]{:S(2)}, u32[]{:S(2)}) collective-permute-start(bf16[1,512,1536]{2,1,0:T(8,128)(2,1)} %get-tuple-element.1262), channel_id=1, source_target_pairs={{0,1},{1,2},{2,3},{3,0},{4,5},{5,6},{6,7},{7,4},{8,9},{9,10},{10,1... | collective-permute-start | bytes 4718600 | tf_op jit(solution)/shard_map/while/body/eval_jaxpr/ppermute | solution.py:151
  1065.7 119.2 %collective-permute-start.14 = (bf16[1,8,64,512]{3,2,1,0:T(8,128)(2,1)}, bf16[1,8,64,512]{3,2,1,0:T(8,128)(2,1)S(1)}, u32[]{:S(2)}, u32[]{:S(2)}) collective-permute-start(bf16[1,8,64,512]{3,2,1,0:T(8,128)(2,1)} %get-tuple-element.1263), channel_id=1, source_target_pairs={{0,1},{1,2},{2,3},{3,0},{4,5},{5,6},{6,7},{7,4},{8,9},{9,10},{10,1... | collective-permute-start | bytes 1572872 | tf_op jit(solution)/shard_map/while/body/eval_jaxpr/ppermute | solution.py:151
  1065.8 113.1 %collective-permute-start.12 = (bf16[1,512]{1,0:T(2,128)(2,1)}, bf16[1,512]{1,0:T(2,128)(2,1)S(1)}, u32[]{:S(2)}, u32[]{:S(2)}) collective-permute-start(bf16[1,512]{1,0:T(2,128)(2,1)} %get-tuple-element.1266), channel_id=1, source_target_pairs={{0,1},{1,2},{2,3},{3,0},{4,5},{5,6},{6,7},{7,4},{8,9},{9,10},{10,1... | collective-permute-start | bytes 3080 | tf_op jit(solution)/shard_map/while/body/eval_jaxpr/ppermute | solution.py:151
  1185.7 92.9 %collective-permute-start.6 = (f32[1,512,1536]{2,1,0:T(8,128)}, f32[1,512,1536]{2,1,0:T(8,128)S(1)}, u32[]{:S(2)}, u32[]{:S(2)}) collective-permute-start(f32[1,512,1536]{2,1,0:T(8,128)} %get-tuple-element.1268), channel_id=1, source_target_pairs={{0,1},{1,2},{2,3},{3,0},{4,5},{5,6},{6,7},{7,4},{8,9},{9,10},{10,1... | collective-permute-start | bytes 9437192 | tf_op jit(solution)/shard_map/while/body/eval_jaxpr/ppermute | solution.py:152
  1185.7 80.8 %collective-permute-start.17 = (bf16[1,2048,512]{2,1,0:T(8,128)(2,1)}, bf16[1,2048,512]{2,1,0:T(8,128)(2,1)}, u32[]{:S(2)}, u32[]{:S(2)}) collective-permute-start(bf16[1,2048,512]{2,1,0:T(8,128)(2,1)} %get-tuple-element.1265), channel_id=1, source_target_pairs={{0,1},{1,2},{2,3},{3,0},{4,5},{5,6},{6,7},{7,4},{8,9},{9,10},{10,1... | collective-permute-start | bytes 6291464 | tf_op jit(solution)/shard_map/while/body/eval_jaxpr/ppermute | solution.py:151
  1378.1 215.1 %collective-permute-start.8 = (f32[1,512,2048]{2,1,0:T(8,128)}, f32[1,512,2048]{2,1,0:T(8,128)}, u32[]{:S(2)}, u32[]{:S(2)}) collective-permute-start(f32[1,512,2048]{2,1,0:T(8,128)} %get-tuple-element.1270), channel_id=1, source_target_pairs={{0,1},{1,2},{2,3},{3,0},{4,5},{5,6},{6,7},{7,4},{8,9},{9,10},{10,1... | collective-permute-start | bytes 12582920 | tf_op jit(solution)/shard_map/while/body/eval_jaxpr/ppermute | solution.py:152
  1378.1 215.1 %collective-permute-start.9 = (f32[1,2048,512]{2,1,0:T(8,128)}, f32[1,2048,512]{2,1,0:T(8,128)}, u32[]{:S(2)}, u32[]{:S(2)}) collective-permute-start(f32[1,2048,512]{2,1,0:T(8,128)} %get-tuple-element.1271), channel_id=1, source_target_pairs={{0,1},{1,2},{2,3},{3,0},{4,5},{5,6},{6,7},{7,4},{8,9},{9,10},{10,1... | collective-permute-start | bytes 12582920 | tf_op jit(solution)/shard_map/while/body/eval_jaxpr/ppermute | solution.py:152
  1378.2 122.1 %collective-permute-start.13 = (bf16[1,512,1536]{2,1,0:T(8,128)(2,1)}, bf16[1,512,1536]{2,1,0:T(8,128)(2,1)}, u32[]{:S(2)}, u32[]{:S(2)}) collective-permute-start(bf16[1,512,1536]{2,1,0:T(8,128)(2,1)} %get-tuple-element.1262), channel_id=1, source_target_pairs={{0,1},{1,2},{2,3},{3,0},{4,5},{5,6},{6,7},{7,4},{8,9},{9,10},{10,1... | collective-permute-start | bytes 4718600 | tf_op jit(solution)/shard_map/while/body/eval_jaxpr/ppermute | solution.py:151
  1380.4 119.1 %collective-permute-start.14 = (bf16[1,8,64,512]{3,2,1,0:T(8,128)(2,1)}, bf16[1,8,64,512]{3,2,1,0:T(8,128)(2,1)S(1)}, u32[]{:S(2)}, u32[]{:S(2)}) collective-permute-start(bf16[1,8,64,512]{3,2,1,0:T(8,128)(2,1)} %get-tuple-element.1263), channel_id=1, source_target_pairs={{0,1},{1,2},{2,3},{3,0},{4,5},{5,6},{6,7},{7,4},{8,9},{9,10},{10,1... | collective-permute-start | bytes 1572872 | tf_op jit(solution)/shard_map/while/body/eval_jaxpr/ppermute | solution.py:151
  1380.4 113.1 %collective-permute-start.12 = (bf16[1,512]{1,0:T(2,128)(2,1)}, bf16[1,512]{1,0:T(2,128)(2,1)S(1)}, u32[]{:S(2)}, u32[]{:S(2)}) collective-permute-start(bf16[1,512]{1,0:T(2,128)(2,1)} %get-tuple-element.1266), channel_id=1, source_target_pairs={{0,1},{1,2},{2,3},{3,0},{4,5},{5,6},{6,7},{7,4},{8,9},{9,10},{10,1... | collective-permute-start | bytes 3080 | tf_op jit(solution)/shard_map/while/body/eval_jaxpr/ppermute | solution.py:151
  1500.3 92.9 %collective-permute-start.6 = (f32[1,512,1536]{2,1,0:T(8,128)}, f32[1,512,1536]{2,1,0:T(8,128)S(1)}, u32[]{:S(2)}, u32[]{:S(2)}) collective-permute-start(f32[1,512,1536]{2,1,0:T(8,128)} %get-tuple-element.1268), channel_id=1, source_target_pairs={{0,1},{1,2},{2,3},{3,0},{4,5},{5,6},{6,7},{7,4},{8,9},{9,10},{10,1... | collective-permute-start | bytes 9437192 | tf_op jit(solution)/shard_map/while/body/eval_jaxpr/ppermute | solution.py:152
  1500.3 80.8 %collective-permute-start.17 = (bf16[1,2048,512]{2,1,0:T(8,128)(2,1)}, bf16[1,2048,512]{2,1,0:T(8,128)(2,1)}, u32[]{:S(2)}, u32[]{:S(2)}) collective-permute-start(bf16[1,2048,512]{2,1,0:T(8,128)(2,1)} %get-tuple-element.1265), channel_id=1, source_target_pairs={{0,1},{1,2},{2,3},{3,0},{4,5},{5,6},{6,7},{7,4},{8,9},{9,10},{10,1... | collective-permute-start | bytes 6291464 | tf_op jit(solution)/shard_map/while/body/eval_jaxpr/ppermute | solution.py:151
  1692.7 215.0 %collective-permute-start.8 = (f32[1,512,2048]{2,1,0:T(8,128)}, f32[1,512,2048]{2,1,0:T(8,128)}, u32[]{:S(2)}, u32[]{:S(2)}) collective-permute-start(f32[1,512,2048]{2,1,0:T(8,128)} %get-tuple-element.1270), channel_id=1, source_target_pairs={{0,1},{1,2},{2,3},{3,0},{4,5},{5,6},{6,7},{7,4},{8,9},{9,10},{10,1... | collective-permute-start | bytes 12582920 | tf_op jit(solution)/shard_map/while/body/eval_jaxpr/ppermute | solution.py:152
  1692.8 215.0 %collective-permute-start.9 = (f32[1,2048,512]{2,1,0:T(8,128)}, f32[1,2048,512]{2,1,0:T(8,128)}, u32[]{:S(2)}, u32[]{:S(2)}) collective-permute-start(f32[1,2048,512]{2,1,0:T(8,128)} %get-tuple-element.1271), channel_id=1, source_target_pairs={{0,1},{1,2},{2,3},{3,0},{4,5},{5,6},{6,7},{7,4},{8,9},{9,10},{10,1... | collective-permute-start | bytes 12582920 | tf_op jit(solution)/shard_map/while/body/eval_jaxpr/ppermute | solution.py:152
  1692.8 122.1 %collective-permute-start.13 = (bf16[1,512,1536]{2,1,0:T(8,128)(2,1)}, bf16[1,512,1536]{2,1,0:T(8,128)(2,1)}, u32[]{:S(2)}, u32[]{:S(2)}) collective-permute-start(bf16[1,512,1536]{2,1,0:T(8,128)(2,1)} %get-tuple-element.1262), channel_id=1, source_target_pairs={{0,1},{1,2},{2,3},{3,0},{4,5},{5,6},{6,7},{7,4},{8,9},{9,10},{10,1... | collective-permute-start | bytes 4718600 | tf_op jit(solution)/shard_map/while/body/eval_jaxpr/ppermute | solution.py:151
  1695.0 119.1 %collective-permute-start.14 = (bf16[1,8,64,512]{3,2,1,0:T(8,128)(2,1)}, bf16[1,8,64,512]{3,2,1,0:T(8,128)(2,1)S(1)}, u32[]{:S(2)}, u32[]{:S(2)}) collective-permute-start(bf16[1,8,64,512]{3,2,1,0:T(8,128)(2,1)} %get-tuple-element.1263), channel_id=1, source_target_pairs={{0,1},{1,2},{2,3},{3,0},{4,5},{5,6},{6,7},{7,4},{8,9},{9,10},{10,1... | collective-permute-start | bytes 1572872 | tf_op jit(solution)/shard_map/while/body/eval_jaxpr/ppermute | solution.py:151
  1695.1 113.1 %collective-permute-start.12 = (bf16[1,512]{1,0:T(2,128)(2,1)}, bf16[1,512]{1,0:T(2,128)(2,1)S(1)}, u32[]{:S(2)}, u32[]{:S(2)}) collective-permute-start(bf16[1,512]{1,0:T(2,128)(2,1)} %get-tuple-element.1266), channel_id=1, source_target_pairs={{0,1},{1,2},{2,3},{3,0},{4,5},{5,6},{6,7},{7,4},{8,9},{9,10},{10,1... | collective-permute-start | bytes 3080 | tf_op jit(solution)/shard_map/while/body/eval_jaxpr/ppermute | solution.py:151
  1814.9 92.9 %collective-permute-start.6 = (f32[1,512,1536]{2,1,0:T(8,128)}, f32[1,512,1536]{2,1,0:T(8,128)S(1)}, u32[]{:S(2)}, u32[]{:S(2)}) collective-permute-start(f32[1,512,1536]{2,1,0:T(8,128)} %get-tuple-element.1268), channel_id=1, source_target_pairs={{0,1},{1,2},{2,3},{3,0},{4,5},{5,6},{6,7},{7,4},{8,9},{9,10},{10,1... | collective-permute-start | bytes 9437192 | tf_op jit(solution)/shard_map/while/body/eval_jaxpr/ppermute | solution.py:152
  1814.9 80.8 %collective-permute-start.17 = (bf16[1,2048,512]{2,1,0:T(8,128)(2,1)}, bf16[1,2048,512]{2,1,0:T(8,128)(2,1)}, u32[]{:S(2)}, u32[]{:S(2)}) collective-permute-start(bf16[1,2048,512]{2,1,0:T(8,128)(2,1)} %get-tuple-element.1265), channel_id=1, source_target_pairs={{0,1},{1,2},{2,3},{3,0},{4,5},{5,6},{6,7},{7,4},{8,9},{9,10},{10,1... | collective-permute-start | bytes 6291464 | tf_op jit(solution)/shard_map/while/body/eval_jaxpr/ppermute | solution.py:151
  2007.4 215.0 %collective-permute-start.8 = (f32[1,512,2048]{2,1,0:T(8,128)}, f32[1,512,2048]{2,1,0:T(8,128)}, u32[]{:S(2)}, u32[]{:S(2)}) collective-permute-start(f32[1,512,2048]{2,1,0:T(8,128)} %get-tuple-element.1270), channel_id=1, source_target_pairs={{0,1},{1,2},{2,3},{3,0},{4,5},{5,6},{6,7},{7,4},{8,9},{9,10},{10,1... | collective-permute-start | bytes 12582920 | tf_op jit(solution)/shard_map/while/body/eval_jaxpr/ppermute | solution.py:152
  2007.4 215.0 %collective-permute-start.9 = (f32[1,2048,512]{2,1,0:T(8,128)}, f32[1,2048,512]{2,1,0:T(8,128)}, u32[]{:S(2)}, u32[]{:S(2)}) collective-permute-start(f32[1,2048,512]{2,1,0:T(8,128)} %get-tuple-element.1271), channel_id=1, source_target_pairs={{0,1},{1,2},{2,3},{3,0},{4,5},{5,6},{6,7},{7,4},{8,9},{9,10},{10,1... | collective-permute-start | bytes 12582920 | tf_op jit(solution)/shard_map/while/body/eval_jaxpr/ppermute | solution.py:152
  2007.4 122.1 %collective-permute-start.13 = (bf16[1,512,1536]{2,1,0:T(8,128)(2,1)}, bf16[1,512,1536]{2,1,0:T(8,128)(2,1)}, u32[]{:S(2)}, u32[]{:S(2)}) collective-permute-start(bf16[1,512,1536]{2,1,0:T(8,128)(2,1)} %get-tuple-element.1262), channel_id=1, source_target_pairs={{0,1},{1,2},{2,3},{3,0},{4,5},{5,6},{6,7},{7,4},{8,9},{9,10},{10,1... | collective-permute-start | bytes 4718600 | tf_op jit(solution)/shard_map/while/body/eval_jaxpr/ppermute | solution.py:151
  2007.5 121.3 %collective-permute-start.14 = (bf16[1,8,64,512]{3,2,1,0:T(8,128)(2,1)}, bf16[1,8,64,512]{3,2,1,0:T(8,128)(2,1)S(1)}, u32[]{:S(2)}, u32[]{:S(2)}) collective-permute-start(bf16[1,8,64,512]{3,2,1,0:T(8,128)(2,1)} %get-tuple-element.1263), channel_id=1, source_target_pairs={{0,1},{1,2},{2,3},{3,0},{4,5},{5,6},{6,7},{7,4},{8,9},{9,10},{10,1... | collective-permute-start | bytes 1572872 | tf_op jit(solution)/shard_map/while/body/eval_jaxpr/ppermute | solution.py:151
  2009.6 113.1 %collective-permute-start.12 = (bf16[1,512]{1,0:T(2,128)(2,1)}, bf16[1,512]{1,0:T(2,128)(2,1)S(1)}, u32[]{:S(2)}, u32[]{:S(2)}) collective-permute-start(bf16[1,512]{1,0:T(2,128)(2,1)} %get-tuple-element.1266), channel_id=1, source_target_pairs={{0,1},{1,2},{2,3},{3,0},{4,5},{5,6},{6,7},{7,4},{8,9},{9,10},{10,1... | collective-permute-start | bytes 3080 | tf_op jit(solution)/shard_map/while/body/eval_jaxpr/ppermute | solution.py:151
  2129.6 92.9 %collective-permute-start.6 = (f32[1,512,1536]{2,1,0:T(8,128)}, f32[1,512,1536]{2,1,0:T(8,128)S(1)}, u32[]{:S(2)}, u32[]{:S(2)}) collective-permute-start(f32[1,512,1536]{2,1,0:T(8,128)} %get-tuple-element.1268), channel_id=1, source_target_pairs={{0,1},{1,2},{2,3},{3,0},{4,5},{5,6},{6,7},{7,4},{8,9},{9,10},{10,1... | collective-permute-start | bytes 9437192 | tf_op jit(solution)/shard_map/while/body/eval_jaxpr/ppermute | solution.py:152
  2129.6 80.8 %collective-permute-start.17 = (bf16[1,2048,512]{2,1,0:T(8,128)(2,1)}, bf16[1,2048,512]{2,1,0:T(8,128)(2,1)}, u32[]{:S(2)}, u32[]{:S(2)}) collective-permute-start(bf16[1,2048,512]{2,1,0:T(8,128)(2,1)} %get-tuple-element.1265), channel_id=1, source_target_pairs={{0,1},{1,2},{2,3},{3,0},{4,5},{5,6},{6,7},{7,4},{8,9},{9,10},{10,1... | collective-permute-start | bytes 6291464 | tf_op jit(solution)/shard_map/while/body/eval_jaxpr/ppermute | solution.py:151
  2237.7 296.6 %collective-permute-start.8 = (f32[1,512,2048]{2,1,0:T(8,128)}, f32[1,512,2048]{2,1,0:T(8,128)}, u32[]{:S(2)}, u32[]{:S(2)}) collective-permute-start(f32[1,512,2048]{2,1,0:T(8,128)} %get-tuple-element.1270), channel_id=1, source_target_pairs={{0,1},{1,2},{2,3},{3,0},{4,5},{5,6},{6,7},{7,4},{8,9},{9,10},{10,1... | collective-permute-start | bytes 12582920 | tf_op jit(solution)/shard_map/while/body/eval_jaxpr/ppermute | solution.py:152
  2321.8 212.6 %collective-permute-start.9 = (f32[1,2048,512]{2,1,0:T(8,128)}, f32[1,2048,512]{2,1,0:T(8,128)}, u32[]{:S(2)}, u32[]{:S(2)}) collective-permute-start(f32[1,2048,512]{2,1,0:T(8,128)} %get-tuple-element.1271), channel_id=1, source_target_pairs={{0,1},{1,2},{2,3},{3,0},{4,5},{5,6},{6,7},{7,4},{8,9},{9,10},{10,1... | collective-permute-start | bytes 12582920 | tf_op jit(solution)/shard_map/while/body/eval_jaxpr/ppermute | solution.py:152
  2321.8 122.1 %collective-permute-start.13 = (bf16[1,512,1536]{2,1,0:T(8,128)(2,1)}, bf16[1,512,1536]{2,1,0:T(8,128)(2,1)}, u32[]{:S(2)}, u32[]{:S(2)}) collective-permute-start(bf16[1,512,1536]{2,1,0:T(8,128)(2,1)} %get-tuple-element.1262), channel_id=1, source_target_pairs={{0,1},{1,2},{2,3},{3,0},{4,5},{5,6},{6,7},{7,4},{8,9},{9,10},{10,1... | collective-permute-start | bytes 4718600 | tf_op jit(solution)/shard_map/while/body/eval_jaxpr/ppermute | solution.py:151
  2321.9 119.0 %collective-permute-start.14 = (bf16[1,8,64,512]{3,2,1,0:T(8,128)(2,1)}, bf16[1,8,64,512]{3,2,1,0:T(8,128)(2,1)S(1)}, u32[]{:S(2)}, u32[]{:S(2)}) collective-permute-start(bf16[1,8,64,512]{3,2,1,0:T(8,128)(2,1)} %get-tuple-element.1263), channel_id=1, source_target_pairs={{0,1},{1,2},{2,3},{3,0},{4,5},{5,6},{6,7},{7,4},{8,9},{9,10},{10,1... | collective-permute-start | bytes 1572872 | tf_op jit(solution)/shard_map/while/body/eval_jaxpr/ppermute | solution.py:151
  2441.7 92.6 %collective-permute-start.6 = (f32[1,512,1536]{2,1,0:T(8,128)}, f32[1,512,1536]{2,1,0:T(8,128)S(1)}, u32[]{:S(2)}, u32[]{:S(2)}) collective-permute-start(f32[1,512,1536]{2,1,0:T(8,128)} %get-tuple-element.1268), channel_id=1, source_target_pairs={{0,1},{1,2},{2,3},{3,0},{4,5},{5,6},{6,7},{7,4},{8,9},{9,10},{10,1... | collective-permute-start | bytes 9437192 | tf_op jit(solution)/shard_map/while/body/eval_jaxpr/ppermute | solution.py:152
  2549.6 275.8 %collective-permute-start.20 = (f32[1,512,2048]{2,1,0:T(8,128)}, f32[1,512,2048]{2,1,0:T(8,128)}, u32[]{:S(2)}, u32[]{:S(2)}) collective-permute-start(f32[1,512,2048]{2,1,0:T(8,128)} %get-tuple-element.747), channel_id=1, source_target_pairs={{0,2},{1,3},{2,0},{3,1},{4,6},{5,7},{6,4},{7,5},{8,10},{9,11},{10,... | collective-permute-start | bytes 12582920 | tf_op jit(solution)/shard_map/ppermute | solution.py:161
  2636.3 189.1 %collective-permute-start.21 = (f32[1,2048,512]{2,1,0:T(8,128)}, f32[1,2048,512]{2,1,0:T(8,128)}, u32[]{:S(2)}, u32[]{:S(2)}) collective-permute-start(f32[1,2048,512]{2,1,0:T(8,128)} %get-tuple-element.748), channel_id=1, source_target_pairs={{0,2},{1,3},{2,0},{3,1},{4,6},{5,7},{6,4},{7,5},{8,10},{9,11},{10,... | collective-permute-start | bytes 12582920 | tf_op jit(solution)/shard_map/ppermute | solution.py:161
  2636.3 188.0 %collective-permute-start.18 = (f32[1,512,1536]{2,1,0:T(8,128)}, f32[1,512,1536]{2,1,0:T(8,128)S(1)}, u32[]{:S(2)}, u32[]{:S(2)}) collective-permute-start(f32[1,512,1536]{2,1,0:T(8,128)} %get-tuple-element.745), channel_id=1, source_target_pairs={{0,2},{1,3},{2,0},{3,1},{4,6},{5,7},{6,4},{7,5},{8,10},{9,11},{10,... | collective-permute-start | bytes 9437192 | tf_op jit(solution)/shard_map/ppermute | solution.py:161
  2638.3 186.1 %collective-permute-start.19 = (f32[1,8,64,512]{3,2,1,0:T(8,128)}, f32[1,8,64,512]{3,2,1,0:T(8,128)S(1)}, u32[]{:S(2)}, u32[]{:S(2)}) collective-permute-start(f32[1,8,64,512]{3,2,1,0:T(8,128)} %get-tuple-element.746), channel_id=1, source_target_pairs={{0,2},{1,3},{2,0},{3,1},{4,6},{5,7},{6,4},{7,5},{8,10},{9,11},{10,... | collective-permute-start | bytes 3145736 | tf_op jit(solution)/shard_map/ppermute | solution.py:161
  (265 other events, 4730.8 us)
Sparse Core Ops, SparseCore 0:
  2827.2 393.8 all-reduce.3
where the time goes:
time: 3250 us; the launch traced here: 3240 us
  waiting for transfers between devices  2100 us (65%)
  starting transfers between devices  372 us (11%)
  local copies, waits for them, and re-layouts  335 us (10%)
  matrix products  292 us (9%)
  other arithmetic  79.7 us (2%)
    ppermute x36, waiting for transfers between devices, bwd_body(): lax.ppermute(w_part, 'pipe', bwd_perm)  1130 us
    ppermute x36, waiting for transfers between devices, fwd_body(): lax.ppermute(w_part, 'pipe', fwd_perm)  401 us
    psum x1, waiting for transfers between devices, device_pass(): grads = tuple((lax.psum(acc_part, 'data') for acc_part in held_acc))  366 us
    while x180, local copies, waits for them, and re-layouts  233 us
    ppermute x6, waiting for transfers between devices, device_pass(): lax.ppermute(acc_part, 'pipe', home_perm)  187 us
    ppermute x36, starting transfers between devices, bwd_body(): lax.ppermute(acc_part, 'pipe', bwd_perm)  119 us
    ppermute x6, starting transfers between devices, device_pass(): lax.ppermute(acc_part, 'pipe', home_perm)  90.9 us
    ppermute x36, starting transfers between devices, bwd_body(): lax.ppermute(w_part, 'pipe', bwd_perm)  84.5 us
  transfers between devices with their start and end apart: 115, of which 46 were waited for; matrix products, arithmetic and copies ran while one was open for 3% of the time, Pallas kernels for 0%

commit v1 on v0

v1 whole, which is shorter than its diff:
```python
import functools
import jax
import jax.numpy as jnp
from jax import lax
from jax.experimental import pallas as pl
from jax.experimental.pallas import tpu as pltpu
from jax.sharding import PartitionSpec as P

NORM_EPS = 1e-5
MESH = pl.DeviceIdType.MESH
F32 = jnp.float32
BF16 = jnp.bfloat16
SEQ = 64
HEAD = 64
D = 512
FFN = 2048
PIPE = 4
SEQ_MB = 3
ROWS = SEQ_MB * SEQ
PAIRS = 4
UNIT = SEQ_MB * PAIRS * SEQ


def dot_nn(lhs, rhs):
    return lax.dot_general(lhs, rhs, (((1,), (0,)), ((), ())), preferred_element_type=F32)


def dot_nt(lhs, rhs):
    return lax.dot_general(lhs, rhs, (((1,), (1,)), ((), ())), preferred_element_type=F32)


def dot_tn(lhs, rhs):
    return lax.dot_general(lhs, rhs, (((0,), (0,)), ((), ())), preferred_element_type=F32)


def pass_kernel(n_mb, acts_ref, cot_ref, lens_ref, wqkv_hbm, wout_hbm, wup_hbm, wdown_hbm, ga_ref, gm_ref,
                out_ref, gqkv_ref, gout_ref, gup_ref, gdown_ref, gga_ref, ggm_ref,
                wqkv, wout, wup, wdown, lens_buf, xin, cin, hout, na_s, qkv_s, ctx_s, mid_s, nm_s, gelu_s, gp_s,
                dpre_s, dmid_s, p_s, s_scr, gstage,
                w_sem, in_sem, x_sem, c_sem, len_sem, send_sem, home_sem, g_sem):
    pos = lax.axis_index('pipe')
    mb_home = n_mb // PIPE
    last = PIPE - 1

    w_copies = [pltpu.make_async_copy(src, dst, w_sem.at[idx]) for idx, (src, dst) in enumerate(
        ((wqkv_hbm, wqkv), (wout_hbm, wout), (wup_hbm, wup), (wdown_hbm, wdown)))]
    for w_copy in w_copies:
        w_copy.start()

    barrier = pltpu.get_barrier_semaphore()
    for step in range(1, PIPE):
        pl.semaphore_signal(barrier, inc=1, device_id={'pipe': (pos + step) % PIPE}, device_id_type=MESH)
    pl.semaphore_wait(barrier, PIPE - 1)

    def rows_of(mb):
        return pl.ds(pl.multiple_of(mb * ROWS, 64), ROWS)

    def place(src, dst, send, recv, target):
        @pl.when(target == pos)
        def _():
            pltpu.make_async_copy(src, dst, recv).start()

        @pl.when(target != pos)
        def _():
            pltpu.make_async_remote_copy(src_ref=src, dst_ref=dst, send_sem=send, recv_sem=recv,
                                         device_id={'pipe': target}, device_id_type=MESH).start()

    def place_done(src, send, target):
        @pl.when(target != pos)
        def _():
            pltpu.make_async_copy(src, src, send).wait()

    n_len = lens_ref.shape[0]
    spread = []
    for half in range(mb_home):
        mb = pos * mb_home + half
        own = pl.ds(half * ROWS, ROWS)
        spread.append((acts_ref.at[own], xin.at[rows_of(mb)], in_sem.at[half], x_sem.at[mb], 0))
        spread.append((cot_ref.at[own], cin.at[rows_of(mb)], in_sem.at[mb_home + half], c_sem.at[mb], last))
    for step in range(PIPE):
        spread.append((lens_ref, lens_buf.at[pl.ds(pos * n_len, n_len)], in_sem.at[2 * mb_home + step], len_sem.at[pos],
                       (pos + step) % PIPE))
    for item in spread:
        place(*item)
    for home in range(PIPE):
        slab = lens_buf.at[pl.ds(home * n_len, n_len)]
        pltpu.make_async_copy(slab, slab, len_sem.at[home]).wait()

    lane = lax.broadcasted_iota(jnp.int32, (SEQ, 128), 1)
    row = lax.broadcasted_iota(jnp.int32, (SEQ, 128), 0)
    first = lane < HEAD
    key_pos = jnp.where(first, lane, lane - HEAD)
    lane_row = lax.broadcasted_iota(jnp.int32, (1, 128), 1)
    take_a = jnp.where(lane_row < HEAD, 1.0, 0.0).astype(BF16)
    take_b = jnp.where(lane_row < HEAD, 0.0, 1.0).astype(BF16)

    def blocks(pair_cols):
        return jnp.concatenate([pair_cols * take_a, pair_cols * take_b], axis=0)

    def halves_sum(arr):
        sum_a = jnp.sum(jnp.where(first[None], arr, 0.0), axis=-1, keepdims=True)
        sum_b = jnp.sum(jnp.where(first[None], 0.0, arr), axis=-1, keepdims=True)
        return sum_a, sum_b

    def lens_of(mb, seq):
        return lens_buf[mb * SEQ_MB + seq][0:1, :]

    def valid_mask(lens_row):
        ok = jnp.where(row < lens_row, 1.0, 0.0)
        return jnp.concatenate([ok] * (D // 128), axis=1)

    def inv_rms(val):
        return lax.rsqrt(jnp.mean(val * val, axis=-1, keepdims=True) + NORM_EPS)

    def forward(mb, _):
        rows = rows_of(mb)
        x_view = xin.at[rows]
        pltpu.make_async_copy(x_view, x_view, x_sem.at[mb]).wait()
        gain_a = ga_ref[...]
        hid = xin[rows, :].astype(F32)
        normed = (hid * inv_rms(hid) * gain_a).astype(BF16)
        na_s[rows, :] = normed
        for part in range(3):
            cols = slice(part * D, (part + 1) * D)
            qkv_s[rows, cols] = dot_nn(normed, wqkv[:, cols]).astype(BF16)

        def seq_rows(seq):
            return pl.ds(pl.multiple_of(mb * ROWS + seq * SEQ, 64), SEQ)

        for seq in range(SEQ_MB):
            for pair in range(PAIRS):
                q_cols = qkv_s[seq_rows(seq), pair * 128:(pair + 1) * 128]
                k_cols = qkv_s[seq_rows(seq), D + pair * 128:D + (pair + 1) * 128]
                spot = (seq * PAIRS + pair) * SEQ
                s_scr[spot:spot + SEQ, :] = dot_nt(q_cols, blocks(k_cols))
        for seq in range(SEQ_MB):
            visible = (key_pos <= row) & (key_pos < lens_of(mb, seq))
            spot = seq * PAIRS * SEQ
            scores = s_scr[spot:spot + PAIRS * SEQ, :].reshape(PAIRS, SEQ, 128) * (HEAD ** -0.5)
            scores = jnp.where(visible[None], scores, -1e30)
            max_a = jnp.max(jnp.where(first[None], scores, -3e38), axis=-1, keepdims=True)
            max_b = jnp.max(jnp.where(first[None], -3e38, scores), axis=-1, keepdims=True)
            expd = jnp.exp(scores - jnp.where(first[None], max_a, max_b))
            sum_a, sum_b = halves_sum(expd)
            probs = expd * jnp.where(first[None], 1.0 / sum_a, 1.0 / sum_b)
            p_rows = pl.ds(pl.multiple_of(mb * UNIT + spot, 64), PAIRS * SEQ)
            p_s[p_rows, :] = probs.reshape(PAIRS * SEQ, 128)
        for seq in range(SEQ_MB):
            for pair in range(PAIRS):
                v_cols = qkv_s[seq_rows(seq), 2 * D + pair * 128:2 * D + (pair + 1) * 128]
                p_rows = pl.ds(pl.multiple_of(mb * UNIT + (seq * PAIRS + pair) * SEQ, 64), SEQ)
                ctx_s[seq_rows(seq), pair * 128:(pair + 1) * 128] = dot_nn(
                    p_s[p_rows, :].astype(BF16), blocks(v_cols)).astype(BF16)
        mid = (hid + dot_nn(ctx_s[rows, :], wout[...])).astype(BF16)
        mid_s[rows, :] = mid
        mid_f = mid.astype(F32)
        normed_m = (mid_f * inv_rms(mid_f) * gm_ref[...]).astype(BF16)
        nm_s[rows, :] = normed_m
        for part in range(FFN // D):
            cols = slice(part * D, (part + 1) * D)
            pre = dot_nn(normed_m, wup[:, cols])
            cdf = 0.5 + 0.5 * lax.erf(pre * (0.5 ** 0.5))
            gelu_s[rows, cols] = (pre * cdf).astype(BF16)
            gp_s[rows, cols] = cdf + pre * (jnp.exp(pre * pre * -0.5) * 0.3989422804014327)
        top = mid_f + dot_nn(gelu_s[rows, :], wdown[...])
        for seq in range(SEQ_MB):
            mask = valid_mask(jnp.where(pos == last, lens_of(mb, seq), SEQ))
            piece = top[seq * SEQ:(seq + 1) * SEQ, :].astype(BF16)
            hout[seq_rows(seq), :] = jnp.where(mask > 0.0, piece.astype(F32), 0.0).astype(BF16)

        h_view = hout.at[rows]

        @pl.when(pos < last)
        def _():
            pltpu.make_async_remote_copy(src_ref=h_view, dst_ref=xin.at[rows], send_sem=send_sem.at[mb],
                                         recv_sem=x_sem.at[mb], device_id={'pipe': pos + 1}, device_id_type=MESH).start()

        @pl.when(pos == last)
        def _():
            half = mb % mb_home
            place(h_view, out_ref.at[pl.ds(pl.multiple_of(half * ROWS, 64), ROWS)], send_sem.at[mb], home_sem.at[half],
                  mb // mb_home)

        return 0

    for w_copy in w_copies:
        w_copy.wait()
    lax.fori_loop(0, n_mb, forward, 0)

    def forward_sent(mb, _):
        h_view = hout.at[rows_of(mb)]

        @pl.when(pos < last)
        def _():
            pltpu.make_async_copy(h_view, h_view, send_sem.at[mb]).wait()

        @pl.when(pos == last)
        def _():
            place_done(h_view, send_sem.at[mb], mb // mb_home)

        return 0

    lax.fori_loop(0, n_mb, forward_sent, 0)
    for half in range(mb_home):
        o_view = out_ref.at[pl.ds(half * ROWS, ROWS)]
        pltpu.make_async_copy(o_view, o_view, home_sem.at[half]).wait()

    gga_ref[...] = jnp.zeros_like(gga_ref)
    ggm_ref[...] = jnp.zeros_like(ggm_ref)

    def norm_back(hid, gain, d_normed):
        inv = inv_rms(hid)
        unit = hid * inv
        d_gain = jnp.sum((d_normed * unit).reshape(ROWS // 8, 8, D), axis=0)
        scaled = d_normed * gain
        return inv * (scaled - unit * jnp.mean(unit * scaled, axis=-1, keepdims=True)), d_gain

    def backward(mb, _):
        rows = rows_of(mb)
        c_view = cin.at[rows]
        pltpu.make_async_copy(c_view, c_view, c_sem.at[mb]).wait()

        def seq_rows(seq):
            return pl.ds(pl.multiple_of(mb * ROWS + seq * SEQ, 64), SEQ)

        for seq in range(SEQ_MB):
            mask = valid_mask(lens_of(mb, seq))
            cin[seq_rows(seq), :] = jnp.where(mask > 0.0, cin[seq_rows(seq), :].astype(F32), 0.0).astype(BF16)
        d_top = cin[rows, :]
        for part in range(FFN // D):
            cols = slice(part * D, (part + 1) * D)
            d_gelu = dot_nt(d_top, wdown[cols, :])
            dpre_s[rows, cols] = (d_gelu * gp_s[rows, cols]).astype(BF16)
        d_nm = dot_nt(dpre_s[rows, :], wup[...])
        d_add, d_gain = norm_back(mid_s[rows, :].astype(F32), gm_ref[...], d_nm)
        ggm_ref[...] += d_gain
        d_mid = d_top.astype(F32) + d_add
        d_mid_bf = d_mid.astype(BF16)
        dmid_s[rows, :] = d_mid_bf
        d_ctx = dot_nt(d_mid_bf, wout[...]).astype(BF16)
        for seq in range(SEQ_MB):
            for pair in range(PAIRS):
                v_cols = qkv_s[seq_rows(seq), 2 * D + pair * 128:2 * D + (pair + 1) * 128]
                dc = d_ctx[seq * SEQ:(seq + 1) * SEQ, pair * 128:(pair + 1) * 128]
                spot = (seq * PAIRS + pair) * SEQ
                p_rows = pl.ds(pl.multiple_of(mb * UNIT + spot, 64), SEQ)
                s_scr[spot:spot + SEQ, :] = dot_nt(dc, blocks(v_cols))
                both = dot_tn(p_s[p_rows, :].astype(BF16), dc)
                qkv_s[seq_rows(seq), 2 * D + pair * 128:2 * D + (pair + 1) * 128] = jnp.where(
                    first, both[:SEQ], both[SEQ:]).astype(BF16)
        for seq in range(SEQ_MB):
            spot = seq * PAIRS * SEQ
            p_rows = pl.ds(pl.multiple_of(mb * UNIT + spot, 64), PAIRS * SEQ)
            probs = p_s[p_rows, :].reshape(PAIRS, SEQ, 128)
            d_probs = s_scr[spot:spot + PAIRS * SEQ, :].reshape(PAIRS, SEQ, 128)
            sum_a, sum_b = halves_sum(probs * d_probs)
            d_scores = probs * (d_probs - jnp.where(first[None], sum_a, sum_b)) * (HEAD ** -0.5)
            s_scr[spot:spot + PAIRS * SEQ, :] = d_scores.reshape(PAIRS * SEQ, 128)
        for seq in range(SEQ_MB):
            for pair in range(PAIRS):
                q_at = slice(pair * 128, (pair + 1) * 128)
                k_at = slice(D + pair * 128, D + (pair + 1) * 128)
                q_cols = qkv_s[seq_rows(seq), q_at]
                k_cols = qkv_s[seq_rows(seq), k_at]
                spot = (seq * PAIRS + pair) * SEQ
                d_sc = s_scr[spot:spot + SEQ, :].astype(BF16)
                both = dot_tn(d_sc, q_cols)
                qkv_s[seq_rows(seq), q_at] = dot_nn(d_sc, blocks(k_cols)).astype(BF16)
                qkv_s[seq_rows(seq), k_at] = jnp.where(first, both[:SEQ], both[SEQ:]).astype(BF16)
        d_na = dot_nt(qkv_s[rows, :], wqkv[...])
        d_add, d_gain = norm_back(xin[rows, :].astype(F32), ga_ref[...], d_na)
        gga_ref[...] += d_gain

        @pl.when(pos > 0)
        def _():
            hout[rows, :] = (d_mid + d_add).astype(BF16)
            pltpu.make_async_remote_copy(src_ref=hout.at[rows], dst_ref=cin.at[rows], send_sem=send_sem.at[mb],
                                         recv_sem=c_sem.at[mb], device_id={'pipe': pos - 1}, device_id_type=MESH).start()

        return 0

    lax.fori_loop(0, n_mb, backward, 0)

    def wgrad(lhs, rhs, dst, n_row, n_col):
        total = n_row * n_col

        def put(tile):
            slot = tile % 2
            at_row = pl.multiple_of((tile // n_col) * 256, 256)
            at_col = pl.multiple_of((tile % n_col) * D, D)
            return pltpu.make_async_copy(gstage.at[slot], dst.at[pl.ds(at_row, 256), pl.ds(at_col, D)], g_sem.at[slot])

        def step(tile, _):
            slot = tile % 2

            @pl.when(tile >= 2)
            def _():
                put(tile - 2).wait()

            at_row = pl.multiple_of((tile // n_col) * 256, 256)
            at_col = pl.multiple_of((tile % n_col) * D, D)
            gstage[slot] = dot_tn(lhs[:, pl.ds(at_row, 256)], rhs[:, pl.ds(at_col, D)])
            put(tile).start()
            return 0

        lax.fori_loop(0, total, step, 0)
        for tile in range(total - 2, total):
            put(tile).wait()

    wgrad(gelu_s, cin, gdown_ref, FFN // 256, 1)
    wgrad(nm_s, dpre_s, gup_ref, D // 256, FFN // D)
    wgrad(ctx_s, dmid_s, gout_ref, D // 256, 1)
    wgrad(na_s, qkv_s, gqkv_ref, D // 256, 3)

    def backward_sent(mb, _):
        @pl.when(pos > 0)
        def _():
            h_view = hout.at[rows_of(mb)]
            pltpu.make_async_copy(h_view, h_view, send_sem.at[mb]).wait()

        return 0

    lax.fori_loop(0, n_mb, backward_sent, 0)
    for src, _, send, _, target in spread:
        place_done(src, send, target)


def run_pass(acts, cots, lens_tile, w_qkv, w_out, w_up, w_down, gain_a, gain_m):
    n_tok = acts.shape[0] * PIPE
    n_mb = n_tok // ROWS
    any_spec = pl.BlockSpec(memory_space=pl.ANY)
    vmem_spec = pl.BlockSpec(memory_space=pltpu.VMEM)
    dma = pltpu.SemaphoreType.DMA
    return pl.pallas_call(
        functools.partial(pass_kernel, n_mb),
        out_shape=(
            jax.ShapeDtypeStruct(acts.shape, BF16),
            jax.ShapeDtypeStruct((D, 3 * D), F32),
            jax.ShapeDtypeStruct((D, D), F32),
            jax.ShapeDtypeStruct((D, FFN), F32),
            jax.ShapeDtypeStruct((FFN, D), F32),
            jax.ShapeDtypeStruct((8, D), F32),
            jax.ShapeDtypeStruct((8, D), F32),
        ),
        in_specs=[any_spec] * 7 + [vmem_spec] * 2,
        out_specs=[any_spec] * 5 + [vmem_spec] * 2,
        scratch_shapes=[
            pltpu.VMEM((D, 3 * D), BF16),
            pltpu.VMEM((D, D), BF16),
            pltpu.VMEM((D, FFN), BF16),
            pltpu.VMEM((FFN, D), BF16),
            pltpu.VMEM((n_mb * SEQ_MB, 8, 128), jnp.int32),
            pltpu.VMEM((n_tok, D), BF16),
            pltpu.VMEM((n_tok, D), BF16),
            pltpu.VMEM((n_tok, D), BF16),
            pltpu.VMEM((n_tok, D), BF16),
            pltpu.VMEM((n_tok, 3 * D), BF16),
            pltpu.VMEM((n_tok, D), BF16),
            pltpu.VMEM((n_tok, D), BF16),
            pltpu.VMEM((n_tok, D), BF16),
            pltpu.VMEM((n_tok, FFN), BF16),
            pltpu.VMEM((n_tok, FFN), F32),
            pltpu.VMEM((n_tok, FFN), BF16),
            pltpu.VMEM((n_tok, D), BF16),
            pltpu.VMEM((n_mb * UNIT, 128), F32),
            pltpu.VMEM((UNIT, 128), F32),
            pltpu.VMEM((2, 256, D), F32),
            dma((4,)),
            dma((2 * (n_mb // PIPE) + PIPE,)),
            dma((n_mb,)),
            dma((n_mb,)),
            dma((PIPE,)),
            dma((n_mb,)),
            dma((n_mb // PIPE,)),
            dma((2,)),
        ],
        compiler_params=pltpu.CompilerParams(collective_id=0, has_side_effects=True, vmem_limit_bytes=64 * 1024 * 1024 - 131072),
    )(acts, cots, lens_tile, w_qkv, w_out, w_up, w_down, gain_a, gain_m)


def solution(mesh):
    row_spec = P(('data', 'pipe'))
    stage_spec = P('pipe')

    def device_pass(acts_in, cot_out, seq_lens, w_qkv, w_out, w_up, w_down, gain_attn, gain_mlp):
        lens_tile = jnp.broadcast_to(seq_lens[:, None, None], (seq_lens.shape[0], 8, 128))
        outs = run_pass(acts_in.reshape(-1, D), cot_out.reshape(-1, D), lens_tile, w_qkv.reshape(D, 3 * D),
                        w_out.reshape(D, D), w_up.reshape(D, FFN), w_down.reshape(FFN, D),
                        gain_attn.astype(F32), gain_mlp.astype(F32))
        acts_out, g_qkv, g_out, g_up, g_down, g_ga, g_gm = outs
        grads = (g_qkv.reshape(w_qkv.shape), g_out.reshape(w_out.shape), g_up.reshape(w_up.shape), g_down.reshape(w_down.shape),
                 jnp.sum(g_ga, axis=0, keepdims=True), jnp.sum(g_gm, axis=0, keepdims=True))
        return (acts_out.reshape(acts_in.shape),) + tuple(lax.psum(part, 'data') for part in grads)

    return jax.shard_map(device_pass, mesh=mesh, in_specs=(row_spec, row_spec, row_spec) + (stage_spec,) * 6, out_specs=(row_spec,) + (stage_spec,) * 6, check_vma=False)
```

time: 3250 us -> 547 us (0.17)
  waiting for transfers between devices: 2100 us -> 369 us
  starting transfers between devices: 372 us -> 0.04 us
  local copies, waits for them, and re-layouts: 335 us -> 13.4 us
  matrix products: 292 us -> 0 us
  Pallas kernels: 0 us -> 125 us
  other arithmetic: 79.7 us -> 2.56 us
    ppermute x114 -> x0, waiting for transfers between devices: 1730 us -> none  [the longest x36 1130 us: bwd_body(): lax.ppermute(w_part, 'pipe', bwd_perm)]
    ppermute x114 -> x0, starting transfers between devices: 372 us -> none  [the longest x36 119 us: bwd_body(): lax.ppermute(acc_part, 'pipe', bwd_perm)]
    dot_general x88 -> x0, matrix products: 292 us -> none  [the longest x16 40.5 us: attention_core(): jnp.einsum('mqhe,mkhe->mhqk', q_heads, k_heads, preferred_element_type=jn...]
    while x180 -> x0, local copies, waits for them, and re-layouts: 233 us -> none
    pallas_call x0 -> x1, Pallas kernels: none -> 125 us  [run_pass(): pl.pallas_call(functools.partial(pass_kernel, n_mb), out_shape=(jax.Shape...]
    reshape x12 -> x0, local copies, waits for them, and re-layouts: 35.3 us -> none  [the longest x8 25.5 us: layer_forward(): qkv_all.astype(jnp.bfloat16).reshape(n_micro, seq_size, 3, heads, head_dim)]
    another operation x8 -> x0, other arithmetic: 33.9 us -> none  [the longest x4 27.1 us: layer_backward(): jax.vjp(functools.partial(jax.nn.gelu, approximate=False), pre_act)[1]]
  transfers between devices with their start and end apart: 115 -> 1, of which waited for: 46 -> 1; matrix products, arithmetic and copies ran while one was open for 3% -> 0% of each run, Pallas kernels for 0% -> 0%
where the time goes in v1:
time: 547 us; the launch traced here: 546 us
  waiting for transfers between devices  369 us (67%)
  Pallas kernels  125 us (23%)
  blocking collectives  22.8 us (4%)
  between operations  14.1 us (3%)
  local copies, waits for them, and re-layouts  13.4 us (2%)
    psum x1, waiting for transfers between devices, device_pass(): lax.psum(part, 'data')  369 us
    pallas_call x1, Pallas kernels, run_pass(): pl.pallas_call(functools.partial(pass_kernel, n_mb), out_shape=(jax.Shape...  125 us
    psum x1, blocking collectives, device_pass(): lax.psum(part, 'data')  22.8 us
    unnamed x17, local copies, waits for them, and re-layouts  12 us
  transfers between devices with their start and end apart: 1, of which 1 were waited for; matrix products, arithmetic and copies ran while one was open for 0% of the time, Pallas kernels for 0%

profile of v1, /device:TPU:0, one launch (start us, length us, event | category | flops | bytes accessed | tf_op | source)
XLA Modules:
  0.0 546.5 jit_solution(9813714692072249518)
XLA Ops:
  7.2 0.0 all-reduce.4.cloned.1.call-start
  7.2 1.3 convert_element_type.6.ga_ref
  8.5 1.3 convert_element_type.7.gm_ref
  9.7 1.3 broadcast_in_dim.12.lens_ref
  11.1 124.6 %shard_map.144 = (bf16[384,512]{1,0:T(8,128)(2,1)}, f32[512,1536]{1,0:T(8,128)}, f32[512,512]{1,0:T(8,128)}, f32[512,2048]{1,0:T(8,128)}, f32[2048,512]{1,0:T(8,...) custom-call(bf16[384,512]{1,0:T(8,128)(2,1)} %bitcast.22, bf16[384,512]{1,0:T(8,128)(2,1)} %bitcast.23, ...), custom_call_target="tpu_custom_call" | custom-call | tf_op jit(solution)/shard_map/pallas_call | solution.py:334
  135.7 0.0 copy-start.5
  135.7 0.0 copy-start.4
  135.7 0.0 copy-start.3
  135.7 0.0 all-reduce.4.cloned.1.call-update
  135.7 0.7 copy-done.5
  136.4 0.0 copy-done.4
  136.4 22.8 %all-reduce = (f32[1,512]{1,0:T(1,128)}, f32[1,512]{1,0:T(1,128)}) all-reduce(f32[1,512]{1,0:T(1,128)S(1)} %bitcast.24, f32[1,512]{1,0:T(1,128)S(1)} %bitcast.25), channel_id=1, replica_groups=mesh['data'=8,'pipe'=4] {'data'}, use_global_device_ids=true, to_apply=%region_5.0 | all-reduce | flops 1024 | bytes 8192 | tf_op jit(solution)/shard_map/psum | solution.py:393
  159.3 369.0 %all-reduce.4.cloned.1.call-done = (f32[1,512,1536]{2,1,0:T(8,128)}, f32[1,8,64,512]{3,2,1,0:T(8,128)}, f32[1,512,2048]{2,1,0:T(8,128)}, f32[1,2048,512]{2,1,0:T(8,128)}) async-done(((f32[1,512,1536]{2,1,0:T(8,128)}, f32[1,8,64,512]{3,2,1,0:T(8,128)}, f32[1,512,2048]{2,1,0:T(8,128)}, f32[1,2048,512]{2,1,0:T(8,128)}), (f32[1,512,1536]{2,1,0:T(8,128)}, f32[1,8,64,512]{3,2,1,0:T(8,128)}, ...) | async-done | bytes 12582928 | tf_op jit(solution)/shard_map/psum | solution.py:393
  528.3 0.0 copy-start.2
  528.3 0.0 copy-done.3
  528.3 0.7 copy.25
  529.0 0.0 copy-start.1
  529.0 3.9 copy.26
  532.9 0.0 copy-done.2
  532.9 1.0 copy.27
  533.9 0.0 copy-done.1
  533.9 0.0 copy-start
  533.9 2.1 copy.28
  536.1 1.6 copy-done
  537.6 2.0 copy.29
  (2 shorter events, 0.0 us)
Async XLA Ops:
  7.2 521.1 %all-reduce.4.cloned.1.call-start = ((), (), s32[]{:S(2)}) async-start(), calls=%async_computation | async-start | bytes 25165824 | tf_op jit(solution)/shard_map/psum | solution.py:393
  135.7 0.7 copy-start.5
  135.7 0.7 copy-start.4
  135.7 392.6 %copy-start.3 = (bf16[384,512]{1,0:T(8,128)(2,1)S(1)}, bf16[384,512]{1,0:T(8,128)(2,1)}, u32[]{:S(2)}) copy-start(bf16[384,512]{1,0:T(8,128)(2,1)} %get-tuple-element.14) | copy-start | bytes 1179652
  528.3 4.7 copy-start.2
  529.0 4.9 copy-start.1
  533.9 3.7 copy-start
Sparse Core Ops, SparseCore 0:
  135.9 392.3 all-reduce.3

commit v2 on v1

--- a/solution.py
+++ b/solution.py
@@ -15,6 +15,12 @@
 D = 512
 FFN = 2048
 PIPE = 4
+DATA = 8
+LINE = 4
+TILE = 128
+UNITS_A = 28
+UNITS_B = 20
+SLOTS = 4
 SEQ_MB = 3
 ROWS = SEQ_MB * SEQ
 PAIRS = 4
@@ -34,11 +40,15 @@
 
 
 def pass_kernel(n_mb, acts_ref, cot_ref, lens_ref, wqkv_hbm, wout_hbm, wup_hbm, wdown_hbm, ga_ref, gm_ref,
-                out_ref, gqkv_ref, gout_ref, gup_ref, gdown_ref, gga_ref, ggm_ref,
+                out_ref, gqkv_ref, gout_ref, gup_ref, gdown_ref, gain_ref,
                 wqkv, wout, wup, wdown, lens_buf, xin, cin, hout, na_s, qkv_s, ctx_s, mid_s, nm_s, gelu_s, gp_s,
-                dpre_s, dmid_s, p_s, s_scr, gstage,
-                w_sem, in_sem, x_sem, c_sem, len_sem, send_sem, home_sem, g_sem):
+                dpre_s, dmid_s, p_s, s_scr, gain_acc, gain_all, ya_buf, la_buf, ra_buf, yb_buf, lb_buf, rb_buf,
+                ya_out, la_out, ra_out, yb_out, lb_out, rb_out,
+                w_sem, in_sem, x_sem, c_sem, len_sem, send_sem, home_sem, sum_recv, sum_send, part_send, gain_recv, gain_send, put_sem):
     pos = lax.axis_index('pipe')
+    rep = lax.axis_index('data')
+    rep_z, rep_y = rep // 2, rep % 2
+    n_tok = n_mb * ROWS
     mb_home = n_mb // PIPE
     last = PIPE - 1
 
@@ -50,10 +60,15 @@
     barrier = pltpu.get_barrier_semaphore()
     for step in range(1, PIPE):
         pl.semaphore_signal(barrier, inc=1, device_id={'pipe': (pos + step) % PIPE}, device_id_type=MESH)
-    pl.semaphore_wait(barrier, PIPE - 1)
+    for step in range(1, DATA):
+        pl.semaphore_signal(barrier, inc=1, device_id={'data': (rep + step) % DATA}, device_id_type=MESH)
+    pl.semaphore_wait(barrier, PIPE - 1 + DATA - 1)
 
     def rows_of(mb):
         return pl.ds(pl.multiple_of(mb * ROWS, 64), ROWS)
+
+    def part_rows(mb, part):
+        return pl.ds(pl.multiple_of(part * n_tok + mb * ROWS, 64), ROWS)
 
     def place(src, dst, send, recv, target):
         @pl.when(target == pos)
@@ -161,7 +176,7 @@
             pre = dot_nn(normed_m, wup[:, cols])
             cdf = 0.5 + 0.5 * lax.erf(pre * (0.5 ** 0.5))
             gelu_s[rows, cols] = (pre * cdf).astype(BF16)
-            gp_s[rows, cols] = cdf + pre * (jnp.exp(pre * pre * -0.5) * 0.3989422804014327)
+            gp_s[part_rows(mb, part), :] = cdf + pre * (jnp.exp(pre * pre * -0.5) * 0.3989422804014327)
         top = mid_f + dot_nn(gelu_s[rows, :], wdown[...])
         for seq in range(SEQ_MB):
             mask = valid_mask(jnp.where(pos == last, lens_of(mb, seq), SEQ))
@@ -205,8 +220,7 @@
         o_view = out_ref.at[pl.ds(half * ROWS, ROWS)]
         pltpu.make_async_copy(o_view, o_view, home_sem.at[half]).wait()
 
-    gga_ref[...] = jnp.zeros_like(gga_ref)
-    ggm_ref[...] = jnp.zeros_like(ggm_ref)
+    gain_acc[...] = jnp.zeros_like(gain_acc)
 
     def norm_back(hid, gain, d_normed):
         inv = inv_rms(hid)
@@ -230,10 +244,10 @@
         for part in range(FFN // D):
             cols = slice(part * D, (part + 1) * D)
             d_gelu = dot_nt(d_top, wdown[cols, :])
-            dpre_s[rows, cols] = (d_gelu * gp_s[rows, cols]).astype(BF16)
+            dpre_s[rows, cols] = (d_gelu * gp_s[part_rows(mb, part), :]).astype(BF16)
         d_nm = dot_nt(dpre_s[rows, :], wup[...])
         d_add, d_gain = norm_back(mid_s[rows, :].astype(F32), gm_ref[...], d_nm)
-        ggm_ref[...] += d_gain
+        gain_acc[1] += d_gain
         d_mid = d_top.astype(F32) + d_add
         d_mid_bf = d_mid.astype(BF16)
         dmid_s[rows, :] = d_mid_bf
@@ -269,7 +283,7 @@
                 qkv_s[seq_rows(seq), k_at] = jnp.where(first, both[:SEQ], both[SEQ:]).astype(BF16)
         d_na = dot_nt(qkv_s[rows, :], wqkv[...])
         d_add, d_gain = norm_back(xin[rows, :].astype(F32), ga_ref[...], d_na)
-        gga_ref[...] += d_gain
+        gain_acc[0] += d_gain
 
         @pl.when(pos > 0)
         def _():
@@ -281,36 +295,247 @@
 
     lax.fori_loop(0, n_mb, backward, 0)
 
-    def wgrad(lhs, rhs, dst, n_row, n_col):
-        total = n_row * n_col
-
-        def put(tile):
-            slot = tile % 2
-            at_row = pl.multiple_of((tile // n_col) * 256, 256)
-            at_col = pl.multiple_of((tile % n_col) * D, D)
-            return pltpu.make_async_copy(gstage.at[slot], dst.at[pl.ds(at_row, 256), pl.ds(at_col, D)], g_sem.at[slot])
-
-        def step(tile, _):
-            slot = tile % 2
-
-            @pl.when(tile >= 2)
-            def _():
-                put(tile - 2).wait()
-
-            at_row = pl.multiple_of((tile // n_col) * 256, 256)
-            at_col = pl.multiple_of((tile % n_col) * D, D)
-            gstage[slot] = dot_tn(lhs[:, pl.ds(at_row, 256)], rhs[:, pl.ds(at_col, D)])
-            put(tile).start()
-            return 0
-
-        lax.fori_loop(0, total, step, 0)
-        for tile in range(total - 2, total):
-            put(tile).wait()
-
-    wgrad(gelu_s, cin, gdown_ref, FFN // 256, 1)
-    wgrad(nm_s, dpre_s, gup_ref, D // 256, FFN // D)
-    wgrad(ctx_s, dmid_s, gout_ref, D // 256, 1)
-    wgrad(na_s, qkv_s, gqkv_ref, D // 256, 3)
+    gain_all[rep] = jnp.concatenate([jnp.sum(gain_acc[0], axis=0, keepdims=True), jnp.sum(gain_acc[1], axis=0, keepdims=True),
+                                     jnp.zeros((6, D), F32)], axis=0)
+    for step in range(1, DATA):
+        pltpu.make_async_remote_copy(src_ref=gain_all.at[rep], dst_ref=gain_all.at[rep], send_sem=gain_send,
+                                     recv_sem=gain_recv.at[rep], device_id={'data': (rep + step) % DATA},
+                                     device_id_type=MESH).start()
+
+    n_down, n_up, n_qkv = FFN // TILE, (D // TILE) * (FFN // D), (D // TILE) * 3
+
+    def tile_kinds(tile):
+        up, qkv, out = tile - n_down, tile - n_down - n_up, tile - n_down - n_up - n_qkv
+        return (
+            (tile < n_down, gelu_s, cin, gdown_ref, tile, 0),
+            ((up >= 0) & (qkv < 0), nm_s, dpre_s, gup_ref, up // (FFN // D), up % (FFN // D)),
+            ((qkv >= 0) & (out < 0), na_s, qkv_s, gqkv_ref, qkv // 3, qkv % 3),
+            (out >= 0, ctx_s, dmid_s, gout_ref, out, 0),
+        )
+
+    def tile_at(tile):
+        return pl.ds(pl.multiple_of(tile * TILE, TILE), TILE)
+
+    def compute_tile(tile):
+        for cond, lhs, rhs, _, at_row, at_col in tile_kinds(tile):
+            @pl.when(cond)
+            def _(lhs=lhs, rhs=rhs, at_row=at_row, at_col=at_col):
+                cols = pl.ds(0, D) if rhs.shape[1] == D else pl.ds(pl.multiple_of(at_col * D, D), D)
+                gp_s[tile_at(tile), :] = dot_tn(lhs[:, pl.ds(pl.multiple_of(at_row * TILE, TILE), TILE)], rhs[:, cols])
+
+    def put_tile(tile):
+        for cond, _, rhs, dst, at_row, at_col in tile_kinds(tile):
+            @pl.when(cond)
+            def _(rhs=rhs, dst=dst, at_row=at_row, at_col=at_col):
+                cols = pl.ds(0, D) if rhs.shape[1] == D else pl.ds(pl.multiple_of(at_col * D, D), D)
+                dst_view = dst.at[pl.ds(pl.multiple_of(at_row * TILE, TILE), TILE), cols]
+                pltpu.make_async_copy(gp_s.at[tile_at(tile)], dst_view, put_sem).start()
+
+    to_y, to_right, to_left = rep + 1 - 2 * rep_y, rep + 2, rep - 2
+
+    def part_done(src, colour, link, slot):
+        pltpu.make_async_copy(src, src, part_send.at[colour, link, slot]).wait()
+
+    def ship_part(unit, slot, src, dst, colour, link, target, value):
+        @pl.when(unit >= SLOTS)
+        def _():
+            part_done(src, colour, link, slot)
+
+        src[...] = value
+        pltpu.make_async_remote_copy(src_ref=src, dst_ref=dst, send_sem=part_send.at[colour, link, slot],
+                                     recv_sem=sum_recv.at[colour, link, slot], device_id={'data': target},
+                                     device_id_type=MESH).start()
+
+    def ship(src, dst, link, recv, target):
+        pltpu.make_async_remote_copy(src_ref=src, dst_ref=dst, send_sem=sum_send.at[link], recv_sem=recv,
+                                     device_id={'data': target}, device_id_type=MESH).start()
+
+    def arrived(view, recv):
+        pltpu.make_async_copy(view, view, recv).wait()
+
+    def gp_rows(start, size):
+        return pl.ds(pl.multiple_of(start, 8), size)
+
+    def line_actions(zz, colour, block, size, buf_l, buf_r, out_l, out_r, hop_rs, hop_ag):
+        chunk = size // LINE
+        own, above = zz * chunk, (zz + 1) * chunk
+
+        def rs_right(unit, slot):
+            at = block(unit)
+            if zz > 0:
+                arrived(buf_l.at[slot, own:size], sum_recv.at[colour, 1, slot])
+                gp_s[gp_rows(at + own, chunk), :] += buf_l[slot, own:above, :]
+            if zz < LINE - 1:
+                value = gp_s[gp_rows(at + above, size - above), :]
+                if zz > 0:
+                    value = value + buf_l[slot, above:size, :]
+                ship_part(unit, slot, out_r.at[slot, above:size], buf_l.at[slot, above:size], colour, 1, to_right, value)
+
+        def rs_left(unit, slot):
+            at = block(unit)
+            if zz < LINE - 1:
+                arrived(buf_r.at[slot, 0:above], sum_recv.at[colour, 2, slot])
+                gp_s[gp_rows(at + own, chunk), :] += buf_r[slot, own:above, :]
+            if zz > 0:
+                value = gp_s[gp_rows(at, own), :]
+                if zz < LINE - 1:
+                    value = value + buf_r[slot, 0:own, :]
+                ship_part(unit, slot, out_l.at[slot, 0:own], buf_r.at[slot, 0:own], colour, 2, to_left, value)
+
+        def ag_right(unit, slot):
+            at = block(unit)
+            if zz > 0:
+                arrived(gp_s.at[gp_rows(at, own)], sum_recv.at[colour, 3, slot])
+            if zz < LINE - 1:
+                view = gp_s.at[gp_rows(at, above)]
+                ship(view, view, 1, sum_recv.at[colour, 3, slot], to_right)
+
+        def ag_left(unit, slot):
+            at = block(unit)
+            if zz < LINE - 1:
+                arrived(gp_s.at[gp_rows(at + above, size - above)], sum_recv.at[colour, 4, slot])
+            if zz > 0:
+                view = gp_s.at[gp_rows(at + own, size - own)]
+                ship(view, view, 2, sum_recv.at[colour, 4, slot], to_left)
+
+        return ([(hop_rs + zz, rs_right), (hop_rs + LINE - 1 - zz, rs_left)],
+                [(hop_ag + zz, ag_right), (hop_ag + LINE - 1 - zz, ag_left)])
+
+    half_a, part_b = TILE // 2, TILE // LINE
+    half_b = part_b // 2
+
+    def actions_a(zz):
+        def mine(unit):
+            return unit * TILE + rep_y * half_a
+
+        def theirs(unit):
+            return unit * TILE + (1 - rep_y) * half_a
+
+        def y_send(unit, slot):
+            ship_part(unit, slot, ya_out.at[slot], ya_buf.at[slot], 0, 0, to_y, gp_s[gp_rows(theirs(unit), half_a), :])
+
+        def y_add(unit, slot):
+            arrived(ya_buf.at[slot], sum_recv.at[0, 0, slot])
+            gp_s[gp_rows(mine(unit), half_a), :] += ya_buf[slot]
+
+        def y_give(unit, slot):
+            view = gp_s.at[gp_rows(mine(unit), half_a)]
+            ship(view, view, 0, sum_recv.at[0, 5, slot], to_y)
+
+        def finish(unit, slot):
+            arrived(gp_s.at[gp_rows(theirs(unit), half_a)], sum_recv.at[0, 5, slot])
+            put_tile(unit)
+
+        scatter, gather = line_actions(zz, 0, mine, half_a, la_buf, ra_buf, la_out, ra_out, 1, 4)
+        return [(0, y_send), (1, y_add)] + scatter + gather + [(7, y_give), (8, finish)]
+
+    def actions_b(zz):
+        def block(unit):
+            return (UNITS_A + unit) * TILE
+
+        def mine(unit):
+            return block(unit) + zz * part_b + rep_y * half_b
+
+        def theirs(unit):
+            return block(unit) + zz * part_b + (1 - rep_y) * half_b
+
+        def y_send(unit, slot):
+            ship_part(unit, slot, yb_out.at[slot], yb_buf.at[slot], 1, 0, to_y, gp_s[gp_rows(theirs(unit), half_b), :])
+
+        def y_add(unit, slot):
+            arrived(yb_buf.at[slot], sum_recv.at[1, 0, slot])
+            gp_s[gp_rows(mine(unit), half_b), :] += yb_buf[slot]
+            view = gp_s.at[gp_rows(mine(unit), half_b)]
+            ship(view, view, 0, sum_recv.at[1, 5, slot], to_y)
+
+        def y_done(unit, slot):
+            arrived(gp_s.at[gp_rows(theirs(unit), half_b)], sum_recv.at[1, 5, slot])
+
+        def finish(unit, slot):
+            put_tile(UNITS_A + unit)
+
+        scatter, gather = line_actions(zz, 1, block, TILE, lb_buf, rb_buf, lb_out, rb_out, 0, 5)
+        return scatter + [(3, y_send), (4, y_add), (5, y_done)] + gather + [(8, finish)]
+
+    def b_unit(tick):
+        unit = tick * UNITS_B // UNITS_A
+        fresh = (tick >= 0) & (tick < UNITS_A) & ((tick + 1) * UNITS_B // UNITS_A > unit)
+        return fresh, unit
+
+    def run_actions(tick, hops):
+        for zz in range(LINE):
+            @pl.when(rep_z == zz)
+            def _(zz=zz):
+                todo = [(hop, 0, fn) for hop, fn in actions_a(zz)] + [(hop, 1, fn) for hop, fn in actions_b(zz)]
+                for want in hops:
+                    for colour in range(2):
+                        fns = [fn for hop, col, fn in todo if hop == want and col == colour]
+                        if not fns:
+                            continue
+                        start = tick - want
+                        if colour == 0:
+                            fresh, unit = (start >= 0) & (start < UNITS_A), start
+                        else:
+                            fresh, unit = b_unit(start)
+
+                        @pl.when(fresh)
+                        def _(fns=fns, unit=unit):
+                            for fn in fns:
+                                fn(unit, unit % SLOTS)
+
+    def compute_for(tick):
+        @pl.when(tick < UNITS_A)
+        def _():
+            compute_tile(tick)
+
+        fresh, unit = b_unit(tick)
+
+        @pl.when(fresh)
+        def _():
+            compute_tile(UNITS_A + unit)
+
+    compute_for(0)
+
+    def tick_step(tick, _):
+        run_actions(tick, [0])
+        compute_for(tick + 1)
+        run_actions(tick, range(1, 9))
+        return 0
+
+    lax.fori_loop(0, UNITS_A + 8, tick_step, 0)
+
+    def sent_all(link, size):
+        view = gp_s.at[pl.ds(0, size)]
+        pltpu.make_async_copy(view, view, sum_send.at[link]).wait()
+
+    for zz in range(LINE):
+        @pl.when(rep_z == zz)
+        def _(zz=zz):
+            line_rows = UNITS_A * (half_a // LINE) + UNITS_B * part_b
+            sent_all(0, UNITS_A * half_a + UNITS_B * half_b)
+            if zz < LINE - 1:
+                sent_all(1, line_rows * (zz + 1))
+            if zz > 0:
+                sent_all(2, line_rows * (LINE - zz))
+            for slot in range(SLOTS):
+                for colour, (out_y, out_l, out_r) in enumerate(((ya_out, la_out, ra_out), (yb_out, lb_out, rb_out))):
+                    size = out_l.shape[1]
+                    part_done(out_y.at[slot], colour, 0, slot)
+                    if zz < LINE - 1:
+                        part_done(out_r.at[slot, (zz + 1) * size // LINE:size], colour, 1, slot)
+                    if zz > 0:
+                        part_done(out_l.at[slot, 0:zz * size // LINE], colour, 2, slot)
+
+    pltpu.make_async_copy(gp_s, gp_s, put_sem).wait()
+
+    for step in range(1, DATA):
+        peer = (rep + step) % DATA
+        pltpu.make_async_copy(gain_all.at[peer], gain_all.at[peer], gain_recv.at[peer]).wait()
+    total = gain_all[0]
+    for peer in range(1, DATA):
+        total = total + gain_all[peer]
+    gain_ref[...] = total
+    pltpu.make_async_copy(gain_all.at[pl.ds(0, DATA - 1)], gain_all.at[pl.ds(0, DATA - 1)], gain_send).wait()
 
     def backward_sent(mb, _):
         @pl.when(pos > 0)
@@ -340,10 +565,9 @@
             jax.ShapeDtypeStruct((D, FFN), F32),
             jax.ShapeDtypeStruct((FFN, D), F32),
             jax.ShapeDtypeStruct((8, D), F32),
-            jax.ShapeDtypeStruct((8, D), F32),
         ),
         in_specs=[any_spec] * 7 + [vmem_spec] * 2,
-        out_specs=[any_spec] * 5 + [vmem_spec] * 2,
+        out_specs=[any_spec] * 5 + [vmem_spec],
         scratch_shapes=[
             pltpu.VMEM((D, 3 * D), BF16),
             pltpu.VMEM((D, D), BF16),
@@ -359,12 +583,17 @@
             pltpu.VMEM((n_tok, D), BF16),
             pltpu.VMEM((n_tok, D), BF16),
             pltpu.VMEM((n_tok, FFN), BF16),
-            pltpu.VMEM((n_tok, FFN), F32),
+            pltpu.VMEM((n_tok * FFN // D, D), F32),
             pltpu.VMEM((n_tok, FFN), BF16),
             pltpu.VMEM((n_tok, D), BF16),
             pltpu.VMEM((n_mb * UNIT, 128), F32),
             pltpu.VMEM((UNIT, 128), F32),
-            pltpu.VMEM((2, 256, D), F32),
+            pltpu.VMEM((2, 8, D), F32),
+            pltpu.VMEM((DATA, 8, D), F32),
+        ] + [
+            pltpu.VMEM((SLOTS, size, D), F32)
+            for size in (TILE // 2, TILE // 2, TILE // 2, TILE // LINE // 2, TILE, TILE) * 2
+        ] + [
             dma((4,)),
             dma((2 * (n_mb // PIPE) + PIPE,)),
             dma((n_mb,)),
@@ -372,7 +601,12 @@
             dma((PIPE,)),
             dma((n_mb,)),
             dma((n_mb // PIPE,)),
-            dma((2,)),
+            dma((2, 6, SLOTS)),
+            dma((3,)),
+            dma((2, 3, SLOTS)),
+            dma((DATA,)),
+            dma,
+            dma,
         ],
         compiler_params=pltpu.CompilerParams(collective_id=0, has_side_effects=True, vmem_limit_bytes=64 * 1024 * 1024 - 131072),
     )(acts, cots, lens_tile, w_qkv, w_out, w_up, w_down, gain_a, gain_m)
@@ -387,9 +621,9 @@
         outs = run_pass(acts_in.reshape(-1, D), cot_out.reshape(-1, D), lens_tile, w_qkv.reshape(D, 3 * D),
                         w_out.reshape(D, D), w_up.reshape(D, FFN), w_down.reshape(FFN, D),
                         gain_attn.astype(F32), gain_mlp.astype(F32))
-        acts_out, g_qkv, g_out, g_up, g_down, g_ga, g_gm = outs
+        acts_out, g_qkv, g_out, g_up, g_down, g_gain = outs
         grads = (g_qkv.reshape(w_qkv.shape), g_out.reshape(w_out.shape), g_up.reshape(w_up.shape), g_down.reshape(w_down.shape),
-                 jnp.sum(g_ga, axis=0, keepdims=True), jnp.sum(g_gm, axis=0, keepdims=True))
-        return (acts_out.reshape(acts_in.shape),) + tuple(lax.psum(part, 'data') for part in grads)
+                 g_gain[0:1], g_gain[1:2])
+        return (acts_out.reshape(acts_in.shape),) + grads
 
     return jax.shard_map(device_pass, mesh=mesh, in_specs=(row_spec, row_spec, row_spec) + (stage_spec,) * 6, out_specs=(row_spec,) + (stage_spec,) * 6, check_vma=False)

time: 547 us -> 348 us (0.64)
  waiting for transfers between devices: 369 us -> 0 us
  Pallas kernels: 125 us -> 329 us
  blocking collectives: 22.8 us -> 0 us
  between operations: 14.1 us -> 0.65 us
    psum x1 -> x0, waiting for transfers between devices: 369 us -> none  [device_pass(): lax.psum(part, 'data')]
    pallas_call x1, Pallas kernels: 125 us -> 329 us  [run_pass(): pl.pallas_call(functools.partial(pass_kernel, n_mb), out_shape=(jax.Shape...]
    psum x1 -> x0, blocking collectives: 22.8 us -> none  [device_pass(): lax.psum(part, 'data')]
    unnamed x17 -> x11, local copies, waits for them, and re-layouts: 12 us -> 12.4 us
  transfers between devices with their start and end apart: 1 -> 0, of which waited for: 1 -> 0; matrix products, arithmetic and copies ran while one was open for 0% -> 0% of each run, Pallas kernels for 0% -> 0%
where the time goes in v2:
time: 348 us
  Pallas kernels  329 us (95%)
  local copies, waits for them, and re-layouts  15.1 us (4%)
    pallas_call x1, Pallas kernels, run_pass(): pl.pallas_call(functools.partial(pass_kernel, n_mb), out_shape=(jax.Shape...  329 us
    unnamed x11, local copies, waits for them, and re-layouts  12.4 us

profile of v2, /device:TPU:0, one launch (start us, length us, event | category | flops | bytes accessed | tf_op | source)
XLA Modules:
  0.0 347.6 jit_solution(17421652921712983673)
XLA Ops:
  0.6 1.3 convert_element_type.6.ga_ref
  1.9 1.3 convert_element_type.7.gm_ref
  3.2 1.3 broadcast_in_dim.2.lens_ref
  4.5 329.3 %shard_map.144 = (bf16[384,512]{1,0:T(8,128)(2,1)}, f32[512,1536]{1,0:T(8,128)}, f32[512,512]{1,0:T(8,128)}, f32[512,2048]{1,0:T(8,128)}, f32[2048,512]{1,0:T(8,128)}, /*index=5*/f32[8,512]{1,0:T(8,128)}) custom-call(bf16[384,512]{1,0:T(8,128)(2,1)} %bitcast.20, bf16[384,512]{1,0:T(8,128)(2,1)} %bitcast.21, s32[6,8,128]{2,1,0:T(8,128)} %broadcast_in_dim.2.lens_ref, ...), custom_call_target="tpu_custom_call" | custom-call | tf_op jit(solution)/shard_map/pallas_call | solution.py:559
  333.8 1.4 fusion
  335.2 1.8 copy.21
  336.9 0.0 copy-start.2
  337.0 0.0 copy-start.1
  337.0 3.9 %copy.22 = f32[1,512,1536]{2,1,0:T(8,128)} copy(f32[1,512,1536]{2,1,0:T(8,128)} %bitcast.13) | data formatting | bytes 6291456
  340.9 0.0 copy-done.2
  340.9 1.0 copy.23
  341.8 0.0 copy-done.1
  341.8 0.0 copy-start
  341.9 2.1 copy.24
  344.0 1.6 copy-done
  345.6 2.0 copy.25
Async XLA Ops:
  336.9 3.9 %copy-start.2 = (f32[512,512]{1,0:T(8,128)S(1)}, f32[512,512]{1,0:T(8,128)}, u32[]{:S(2)}) copy-start(f32[512,512]{1,0:T(8,128)} %get-tuple-element.15) | copy-start | bytes 3145732
  337.0 4.9 %copy-start.1 = (f32[512,2048]{1,0:T(8,128)S(1)}, f32[512,2048]{1,0:T(8,128)}, u32[]{:S(2)}) copy-start(f32[512,2048]{1,0:T(8,128)} %get-tuple-element.16) | copy-start | bytes 12582916
  341.8 3.7 %copy-start = (f32[2048,512]{1,0:T(8,128)S(1)}, f32[2048,512]{1,0:T(8,128)}, u32[]{:S(2)}) copy-start(f32[2048,512]{1,0:T(8,128)} %get-tuple-element.17) | copy-start | bytes 12582916

commit v3 on v2

--- a/solution.py
+++ b/solution.py
@@ -18,13 +18,12 @@
 DATA = 8
 LINE = 4
 TILE = 128
-UNITS_A = 28
-UNITS_B = 20
+PART = 64
+UNITS_A = 56
+UNITS_B = 40
 SLOTS = 4
 SEQ_MB = 3
-ROWS = SEQ_MB * SEQ
 PAIRS = 4
-UNIT = SEQ_MB * PAIRS * SEQ
 
 
 def dot_nn(lhs, rhs):
@@ -39,7 +38,7 @@
     return lax.dot_general(lhs, rhs, (((0,), (0,)), ((), ())), preferred_element_type=F32)
 
 
-def pass_kernel(n_mb, acts_ref, cot_ref, lens_ref, wqkv_hbm, wout_hbm, wup_hbm, wdown_hbm, ga_ref, gm_ref,
+def pass_kernel(n_seq, acts_ref, cot_ref, lens_ref, wqkv_hbm, wout_hbm, wup_hbm, wdown_hbm, ga_ref, gm_ref,
                 out_ref, gqkv_ref, gout_ref, gup_ref, gdown_ref, gain_ref,
                 wqkv, wout, wup, wdown, lens_buf, xin, cin, hout, na_s, qkv_s, ctx_s, mid_s, nm_s, gelu_s, gp_s,
                 dpre_s, dmid_s, p_s, s_scr, gain_acc, gain_all, ya_buf, la_buf, ra_buf, yb_buf, lb_buf, rb_buf,
@@ -48,8 +47,12 @@
     pos = lax.axis_index('pipe')
     rep = lax.axis_index('data')
     rep_z, rep_y = rep // 2, rep % 2
-    n_tok = n_mb * ROWS
-    mb_home = n_mb // PIPE
+    n_tok = n_seq * SEQ
+    n_mb = n_seq // SEQ_MB + SEQ_MB - 1
+    n_own = n_seq // PIPE
+    own_slab = pl.ds(pos * n_own, n_own)
+    for seq in range(n_own):
+        lens_buf[pos * n_own + seq] = jnp.full((8, 128), lens_ref[seq], jnp.int32)
     last = PIPE - 1
 
     w_copies = [pltpu.make_async_copy(src, dst, w_sem.at[idx]) for idx, (src, dst) in enumerate(
@@ -64,11 +67,21 @@
         pl.semaphore_signal(barrier, inc=1, device_id={'data': (rep + step) % DATA}, device_id_type=MESH)
     pl.semaphore_wait(barrier, PIPE - 1 + DATA - 1)
 
-    def rows_of(mb):
-        return pl.ds(pl.multiple_of(mb * ROWS, 64), ROWS)
-
-    def part_rows(mb, part):
-        return pl.ds(pl.multiple_of(part * n_tok + mb * ROWS, 64), ROWS)
+    def first_seq(mb, size):
+        return mb if size == 1 else (mb - SEQ_MB + 1) * SEQ_MB
+
+    def rows_of(mb, size):
+        return pl.ds(pl.multiple_of(first_seq(mb, size) * SEQ, SEQ), size * SEQ)
+
+    def seq_rows(mb, size, seq):
+        return pl.ds(pl.multiple_of((first_seq(mb, size) + seq) * SEQ, SEQ), SEQ)
+
+    def part_rows(mb, size, part):
+        return pl.ds(pl.multiple_of(part * n_tok + first_seq(mb, size) * SEQ, SEQ), size * SEQ)
+
+    def send_to(src, dst, send, recv, target):
+        pltpu.make_async_remote_copy(src_ref=src, dst_ref=dst, send_sem=send, recv_sem=recv,
+                                     device_id={'pipe': target}, device_id_type=MESH).start()
 
     def place(src, dst, send, recv, target):
         @pl.when(target == pos)
@@ -77,29 +90,19 @@
 
         @pl.when(target != pos)
         def _():
-            pltpu.make_async_remote_copy(src_ref=src, dst_ref=dst, send_sem=send, recv_sem=recv,
-                                         device_id={'pipe': target}, device_id_type=MESH).start()
-
-    def place_done(src, send, target):
-        @pl.when(target != pos)
-        def _():
-            pltpu.make_async_copy(src, src, send).wait()
-
-    n_len = lens_ref.shape[0]
+            send_to(src, dst, send, recv, target)
+
+    for step in range(1, PIPE):
+        send_to(lens_buf.at[own_slab], lens_buf.at[own_slab], in_sem.at[step - 1], len_sem.at[pos], (pos + step) % PIPE)
     spread = []
-    for half in range(mb_home):
-        mb = pos * mb_home + half
-        own = pl.ds(half * ROWS, ROWS)
-        spread.append((acts_ref.at[own], xin.at[rows_of(mb)], in_sem.at[half], x_sem.at[mb], 0))
-        spread.append((cot_ref.at[own], cin.at[rows_of(mb)], in_sem.at[mb_home + half], c_sem.at[mb], last))
-    for step in range(PIPE):
-        spread.append((lens_ref, lens_buf.at[pl.ds(pos * n_len, n_len)], in_sem.at[2 * mb_home + step], len_sem.at[pos],
-                       (pos + step) % PIPE))
+    for src, dst, sem, target in ((acts_ref, xin, x_sem, 0), (cot_ref, cin, c_sem, last)):
+        for seq in range(n_own):
+            at = pos * n_own + seq
+            mb = jnp.where(at < SEQ_MB, at, at // SEQ_MB + SEQ_MB - 1)
+            spread.append((src.at[pl.ds(seq * SEQ, SEQ)], dst.at[pl.ds(pl.multiple_of(at * SEQ, SEQ), SEQ)],
+                           in_sem.at[PIPE - 1 + len(spread)], sem.at[mb], target))
     for item in spread:
         place(*item)
-    for home in range(PIPE):
-        slab = lens_buf.at[pl.ds(home * n_len, n_len)]
-        pltpu.make_async_copy(slab, slab, len_sem.at[home]).wait()
 
     lane = lax.broadcasted_iota(jnp.int32, (SEQ, 128), 1)
     row = lax.broadcasted_iota(jnp.int32, (SEQ, 128), 0)
@@ -117,8 +120,8 @@
         sum_b = jnp.sum(jnp.where(first[None], 0.0, arr), axis=-1, keepdims=True)
         return sum_a, sum_b
 
-    def lens_of(mb, seq):
-        return lens_buf[mb * SEQ_MB + seq][0:1, :]
+    def lens_of(mb, size, seq):
+        return lens_buf[first_seq(mb, size) + seq][0:1, :]
 
     def valid_mask(lens_row):
         ok = jnp.where(row < lens_row, 1.0, 0.0)
@@ -127,11 +130,18 @@
     def inv_rms(val):
         return lax.rsqrt(jnp.mean(val * val, axis=-1, keepdims=True) + NORM_EPS)
 
-    def forward(mb, _):
-        rows = rows_of(mb)
+    def forward(size, mb, _):
+        rows = rows_of(mb, size)
+        start = first_seq(mb, size)
+
+        @pl.when((start % n_own == 0) & (start // n_own != pos))
+        def _():
+            slab = lens_buf.at[pl.ds(start, n_own)]
+            pltpu.make_async_copy(slab, slab, len_sem.at[start // n_own]).wait()
+
         x_view = xin.at[rows]
         pltpu.make_async_copy(x_view, x_view, x_sem.at[mb]).wait()
-        gain_a = ga_ref[...]
+        gain_a = ga_ref[...].astype(F32)
         hid = xin[rows, :].astype(F32)
         normed = (hid * inv_rms(hid) * gain_a).astype(BF16)
         na_s[rows, :] = normed
@@ -139,17 +149,14 @@
             cols = slice(part * D, (part + 1) * D)
             qkv_s[rows, cols] = dot_nn(normed, wqkv[:, cols]).astype(BF16)
 
-        def seq_rows(seq):
-            return pl.ds(pl.multiple_of(mb * ROWS + seq * SEQ, 64), SEQ)
-
-        for seq in range(SEQ_MB):
+        for seq in range(size):
             for pair in range(PAIRS):
-                q_cols = qkv_s[seq_rows(seq), pair * 128:(pair + 1) * 128]
-                k_cols = qkv_s[seq_rows(seq), D + pair * 128:D + (pair + 1) * 128]
+                q_cols = qkv_s[seq_rows(mb, size, seq), pair * 128:(pair + 1) * 128]
+                k_cols = qkv_s[seq_rows(mb, size, seq), D + pair * 128:D + (pair + 1) * 128]
                 spot = (seq * PAIRS + pair) * SEQ
                 s_scr[spot:spot + SEQ, :] = dot_nt(q_cols, blocks(k_cols))
-        for seq in range(SEQ_MB):
-            visible = (key_pos <= row) & (key_pos < lens_of(mb, seq))
+        for seq in range(size):
+            visible = (key_pos <= row) & (key_pos < lens_of(mb, size, seq))
             spot = seq * PAIRS * SEQ
             scores = s_scr[spot:spot + PAIRS * SEQ, :].reshape(PAIRS, SEQ, 128) * (HEAD ** -0.5)
             scores = jnp.where(visible[None], scores, -1e30)
@@ -158,142 +165,135 @@
             expd = jnp.exp(scores - jnp.where(first[None], max_a, max_b))
             sum_a, sum_b = halves_sum(expd)
             probs = expd * jnp.where(first[None], 1.0 / sum_a, 1.0 / sum_b)
-            p_rows = pl.ds(pl.multiple_of(mb * UNIT + spot, 64), PAIRS * SEQ)
+            p_rows = pl.ds(pl.multiple_of(start * PAIRS * SEQ + spot, SEQ), PAIRS * SEQ)
             p_s[p_rows, :] = probs.reshape(PAIRS * SEQ, 128)
-        for seq in range(SEQ_MB):
+        for seq in range(size):
             for pair in range(PAIRS):
-                v_cols = qkv_s[seq_rows(seq), 2 * D + pair * 128:2 * D + (pair + 1) * 128]
-                p_rows = pl.ds(pl.multiple_of(mb * UNIT + (seq * PAIRS + pair) * SEQ, 64), SEQ)
-                ctx_s[seq_rows(seq), pair * 128:(pair + 1) * 128] = dot_nn(
+                v_cols = qkv_s[seq_rows(mb, size, seq), 2 * D + pair * 128:2 * D + (pair + 1) * 128]
+                p_rows = pl.ds(pl.multiple_of((start * PAIRS + seq * PAIRS + pair) * SEQ, SEQ), SEQ)
+                ctx_s[seq_rows(mb, size, seq), pair * 128:(pair + 1) * 128] = dot_nn(
                     p_s[p_rows, :].astype(BF16), blocks(v_cols)).astype(BF16)
         mid = (hid + dot_nn(ctx_s[rows, :], wout[...])).astype(BF16)
         mid_s[rows, :] = mid
         mid_f = mid.astype(F32)
-        normed_m = (mid_f * inv_rms(mid_f) * gm_ref[...]).astype(BF16)
+        normed_m = (mid_f * inv_rms(mid_f) * gm_ref[...].astype(F32)).astype(BF16)
         nm_s[rows, :] = normed_m
         for part in range(FFN // D):
             cols = slice(part * D, (part + 1) * D)
             pre = dot_nn(normed_m, wup[:, cols])
             cdf = 0.5 + 0.5 * lax.erf(pre * (0.5 ** 0.5))
             gelu_s[rows, cols] = (pre * cdf).astype(BF16)
-            gp_s[part_rows(mb, part), :] = cdf + pre * (jnp.exp(pre * pre * -0.5) * 0.3989422804014327)
+            gp_s[part_rows(mb, size, part), :] = cdf + pre * (jnp.exp(pre * pre * -0.5) * 0.3989422804014327)
         top = mid_f + dot_nn(gelu_s[rows, :], wdown[...])
-        for seq in range(SEQ_MB):
-            mask = valid_mask(jnp.where(pos == last, lens_of(mb, seq), SEQ))
+        for seq in range(size):
+            mask = valid_mask(jnp.where(pos == last, lens_of(mb, size, seq), SEQ))
             piece = top[seq * SEQ:(seq + 1) * SEQ, :].astype(BF16)
-            hout[seq_rows(seq), :] = jnp.where(mask > 0.0, piece.astype(F32), 0.0).astype(BF16)
+            hout[seq_rows(mb, size, seq), :] = jnp.where(mask > 0.0, piece.astype(F32), 0.0).astype(BF16)
 
         h_view = hout.at[rows]
 
         @pl.when(pos < last)
         def _():
-            pltpu.make_async_remote_copy(src_ref=h_view, dst_ref=xin.at[rows], send_sem=send_sem.at[mb],
-                                         recv_sem=x_sem.at[mb], device_id={'pipe': pos + 1}, device_id_type=MESH).start()
+            send_to(h_view, xin.at[rows], send_sem.at[mb], x_sem.at[mb], pos + 1)
 
         @pl.when(pos == last)
         def _():
-            half = mb % mb_home
-            place(h_view, out_ref.at[pl.ds(pl.multiple_of(half * ROWS, 64), ROWS)], send_sem.at[mb], home_sem.at[half],
-                  mb // mb_home)
+            home = start // n_own
+            o_view = out_ref.at[pl.ds(pl.multiple_of((start % n_own) * SEQ, SEQ), size * SEQ)]
+
+            @pl.when(home == pos)
+            def _():
+                pltpu.make_async_copy(h_view, o_view, send_sem.at[mb]).start()
+
+            @pl.when(home != pos)
+            def _():
+                send_to(h_view, o_view, send_sem.at[mb], home_sem, home)
 
         return 0
 
     for w_copy in w_copies:
         w_copy.wait()
-    lax.fori_loop(0, n_mb, forward, 0)
-
-    def forward_sent(mb, _):
-        h_view = hout.at[rows_of(mb)]
-
-        @pl.when(pos < last)
-        def _():
-            pltpu.make_async_copy(h_view, h_view, send_sem.at[mb]).wait()
-
-        @pl.when(pos == last)
-        def _():
-            place_done(h_view, send_sem.at[mb], mb // mb_home)
-
+    lax.fori_loop(0, SEQ_MB, functools.partial(forward, 1), 0)
+    lax.fori_loop(SEQ_MB, n_mb, functools.partial(forward, SEQ_MB), 0)
+
+    def sent(size, mb, _):
+        h_view = hout.at[rows_of(mb, size)]
+        pltpu.make_async_copy(h_view, h_view, send_sem.at[mb]).wait()
         return 0
-
-    lax.fori_loop(0, n_mb, forward_sent, 0)
-    for half in range(mb_home):
-        o_view = out_ref.at[pl.ds(half * ROWS, ROWS)]
-        pltpu.make_async_copy(o_view, o_view, home_sem.at[half]).wait()
 
     gain_acc[...] = jnp.zeros_like(gain_acc)
 
     def norm_back(hid, gain, d_normed):
         inv = inv_rms(hid)
         unit = hid * inv
-        d_gain = jnp.sum((d_normed * unit).reshape(ROWS // 8, 8, D), axis=0)
+        d_gain = jnp.sum((d_normed * unit).reshape(hid.shape[0] // 8, 8, D), axis=0)
         scaled = d_normed * gain
         return inv * (scaled - unit * jnp.mean(unit * scaled, axis=-1, keepdims=True)), d_gain
 
-    def backward(mb, _):
-        rows = rows_of(mb)
+    def backward(size, mb, _):
+        rows = rows_of(mb, size)
+        start = first_seq(mb, size)
         c_view = cin.at[rows]
         pltpu.make_async_copy(c_view, c_view, c_sem.at[mb]).wait()
 
-        def seq_rows(seq):
-            return pl.ds(pl.multiple_of(mb * ROWS + seq * SEQ, 64), SEQ)
-
-        for seq in range(SEQ_MB):
-            mask = valid_mask(lens_of(mb, seq))
-            cin[seq_rows(seq), :] = jnp.where(mask > 0.0, cin[seq_rows(seq), :].astype(F32), 0.0).astype(BF16)
+        for seq in range(size):
+            mask = valid_mask(lens_of(mb, size, seq))
+            cin[seq_rows(mb, size, seq), :] = jnp.where(mask > 0.0, cin[seq_rows(mb, size, seq), :].astype(F32), 0.0).astype(BF16)
         d_top = cin[rows, :]
         for part in range(FFN // D):
             cols = slice(part * D, (part + 1) * D)
             d_gelu = dot_nt(d_top, wdown[cols, :])
-            dpre_s[rows, cols] = (d_gelu * gp_s[part_rows(mb, part), :]).astype(BF16)
+            dpre_s[rows, cols] = (d_gelu * gp_s[part_rows(mb, size, part), :]).astype(BF16)
         d_nm = dot_nt(dpre_s[rows, :], wup[...])
-        d_add, d_gain = norm_back(mid_s[rows, :].astype(F32), gm_ref[...], d_nm)
+        d_add, d_gain = norm_back(mid_s[rows, :].astype(F32), gm_ref[...].astype(F32), d_nm)
         gain_acc[1] += d_gain
         d_mid = d_top.astype(F32) + d_add
         d_mid_bf = d_mid.astype(BF16)
         dmid_s[rows, :] = d_mid_bf
         d_ctx = dot_nt(d_mid_bf, wout[...]).astype(BF16)
-        for seq in range(SEQ_MB):
+        for seq in range(size):
             for pair in range(PAIRS):
-                v_cols = qkv_s[seq_rows(seq), 2 * D + pair * 128:2 * D + (pair + 1) * 128]
+                v_cols = qkv_s[seq_rows(mb, size, seq), 2 * D + pair * 128:2 * D + (pair + 1) * 128]
                 dc = d_ctx[seq * SEQ:(seq + 1) * SEQ, pair * 128:(pair + 1) * 128]
                 spot = (seq * PAIRS + pair) * SEQ
-                p_rows = pl.ds(pl.multiple_of(mb * UNIT + spot, 64), SEQ)
+                p_rows = pl.ds(pl.multiple_of(start * PAIRS * SEQ + spot, SEQ), SEQ)
                 s_scr[spot:spot + SEQ, :] = dot_nt(dc, blocks(v_cols))
                 both = dot_tn(p_s[p_rows, :].astype(BF16), dc)
-                qkv_s[seq_rows(seq), 2 * D + pair * 128:2 * D + (pair + 1) * 128] = jnp.where(
+                qkv_s[seq_rows(mb, size, seq), 2 * D + pair * 128:2 * D + (pair + 1) * 128] = jnp.where(
                     first, both[:SEQ], both[SEQ:]).astype(BF16)
-        for seq in range(SEQ_MB):
+        for seq in range(size):
             spot = seq * PAIRS * SEQ
-            p_rows = pl.ds(pl.multiple_of(mb * UNIT + spot, 64), PAIRS * SEQ)
+            p_rows = pl.ds(pl.multiple_of(start * PAIRS * SEQ + spot, SEQ), PAIRS * SEQ)
             probs = p_s[p_rows, :].reshape(PAIRS, SEQ, 128)
             d_probs = s_scr[spot:spot + PAIRS * SEQ, :].reshape(PAIRS, SEQ, 128)
             sum_a, sum_b = halves_sum(probs * d_probs)
             d_scores = probs * (d_probs - jnp.where(first[None], sum_a, sum_b)) * (HEAD ** -0.5)
             s_scr[spot:spot + PAIRS * SEQ, :] = d_scores.reshape(PAIRS * SEQ, 128)
-        for seq in range(SEQ_MB):
+        for seq in range(size):
             for pair in range(PAIRS):
                 q_at = slice(pair * 128, (pair + 1) * 128)
                 k_at = slice(D + pair * 128, D + (pair + 1) * 128)
-                q_cols = qkv_s[seq_rows(seq), q_at]
-                k_cols = qkv_s[seq_rows(seq), k_at]
+                q_cols = qkv_s[seq_rows(mb, size, seq), q_at]
+                k_cols = qkv_s[seq_rows(mb, size, seq), k_at]
                 spot = (seq * PAIRS + pair) * SEQ
                 d_sc = s_scr[spot:spot + SEQ, :].astype(BF16)
                 both = dot_tn(d_sc, q_cols)
-                qkv_s[seq_rows(seq), q_at] = dot_nn(d_sc, blocks(k_cols)).astype(BF16)
-                qkv_s[seq_rows(seq), k_at] = jnp.where(first, both[:SEQ], both[SEQ:]).astype(BF16)
+                qkv_s[seq_rows(mb, size, seq), q_at] = dot_nn(d_sc, blocks(k_cols)).astype(BF16)
+                qkv_s[seq_rows(mb, size, seq), k_at] = jnp.where(first, both[:SEQ], both[SEQ:]).astype(BF16)
         d_na = dot_nt(qkv_s[rows, :], wqkv[...])
-        d_add, d_gain = norm_back(xin[rows, :].astype(F32), ga_ref[...], d_na)
+        d_add, d_gain = norm_back(xin[rows, :].astype(F32), ga_ref[...].astype(F32), d_na)
         gain_acc[0] += d_gain
 
         @pl.when(pos > 0)
         def _():
+            sent(size, mb, 0)
             hout[rows, :] = (d_mid + d_add).astype(BF16)
-            pltpu.make_async_remote_copy(src_ref=hout.at[rows], dst_ref=cin.at[rows], send_sem=send_sem.at[mb],
-                                         recv_sem=c_sem.at[mb], device_id={'pipe': pos - 1}, device_id_type=MESH).start()
+            send_to(hout.at[rows], cin.at[rows], send_sem.at[mb], c_sem.at[mb], pos - 1)
 
         return 0
 
-    lax.fori_loop(0, n_mb, backward, 0)
+    lax.fori_loop(SEQ_MB, n_mb, functools.partial(backward, SEQ_MB), 0)
+    lax.fori_loop(0, SEQ_MB, functools.partial(backward, 1), 0)
 
     gain_all[rep] = jnp.concatenate([jnp.sum(gain_acc[0], axis=0, keepdims=True), jnp.sum(gain_acc[1], axis=0, keepdims=True),
                                      jnp.zeros((6, D), F32)], axis=0)
@@ -302,6 +302,7 @@
                                      recv_sem=gain_recv.at[rep], device_id={'data': (rep + step) % DATA},
                                      device_id_type=MESH).start()
 
+    per_tile = TILE // PART
     n_down, n_up, n_qkv = FFN // TILE, (D // TILE) * (FFN // D), (D // TILE) * 3
 
     def tile_kinds(tile):
@@ -323,13 +324,13 @@
                 cols = pl.ds(0, D) if rhs.shape[1] == D else pl.ds(pl.multiple_of(at_col * D, D), D)
                 gp_s[tile_at(tile), :] = dot_tn(lhs[:, pl.ds(pl.multiple_of(at_row * TILE, TILE), TILE)], rhs[:, cols])
 
-    def put_tile(tile):
-        for cond, _, rhs, dst, at_row, at_col in tile_kinds(tile):
+    def put_unit(unit):
+        for cond, _, rhs, dst, at_row, at_col in tile_kinds(unit // per_tile):
             @pl.when(cond)
             def _(rhs=rhs, dst=dst, at_row=at_row, at_col=at_col):
                 cols = pl.ds(0, D) if rhs.shape[1] == D else pl.ds(pl.multiple_of(at_col * D, D), D)
-                dst_view = dst.at[pl.ds(pl.multiple_of(at_row * TILE, TILE), TILE), cols]
-                pltpu.make_async_copy(gp_s.at[tile_at(tile)], dst_view, put_sem).start()
+                dst_view = dst.at[pl.ds(pl.multiple_of(at_row * TILE + (unit % per_tile) * PART, PART), PART), cols]
+                pltpu.make_async_copy(gp_s.at[gp_rows(unit * PART, PART)], dst_view, put_sem).start()
 
     to_y, to_right, to_left = rep + 1 - 2 * rep_y, rep + 2, rep - 2
 
@@ -401,15 +402,15 @@
         return ([(hop_rs + zz, rs_right), (hop_rs + LINE - 1 - zz, rs_left)],
                 [(hop_ag + zz, ag_right), (hop_ag + LINE - 1 - zz, ag_left)])
 
-    half_a, part_b = TILE // 2, TILE // LINE
+    half_a, part_b = PART // 2, PART // LINE
     half_b = part_b // 2
 
     def actions_a(zz):
         def mine(unit):
-            return unit * TILE + rep_y * half_a
+            return unit * PART + rep_y * half_a
 
         def theirs(unit):
-            return unit * TILE + (1 - rep_y) * half_a
+            return unit * PART + (1 - rep_y) * half_a
 
         def y_send(unit, slot):
             ship_part(unit, slot, ya_out.at[slot], ya_buf.at[slot], 0, 0, to_y, gp_s[gp_rows(theirs(unit), half_a), :])
@@ -424,14 +425,14 @@
 
         def finish(unit, slot):
             arrived(gp_s.at[gp_rows(theirs(unit), half_a)], sum_recv.at[0, 5, slot])
-            put_tile(unit)
+            put_unit(unit)
 
         scatter, gather = line_actions(zz, 0, mine, half_a, la_buf, ra_buf, la_out, ra_out, 1, 4)
         return [(0, y_send), (1, y_add)] + scatter + gather + [(7, y_give), (8, finish)]
 
     def actions_b(zz):
         def block(unit):
-            return (UNITS_A + unit) * TILE
+            return (UNITS_A + unit) * PART
 
         def mine(unit):
             return block(unit) + zz * part_b + rep_y * half_b
@@ -452,9 +453,9 @@
             arrived(gp_s.at[gp_rows(theirs(unit), half_b)], sum_recv.at[1, 5, slot])
 
         def finish(unit, slot):
-            put_tile(UNITS_A + unit)
-
-        scatter, gather = line_actions(zz, 1, block, TILE, lb_buf, rb_buf, lb_out, rb_out, 0, 5)
+            put_unit(UNITS_A + unit)
+
+        scatter, gather = line_actions(zz, 1, block, PART, lb_buf, rb_buf, lb_out, rb_out, 0, 5)
         return scatter + [(3, y_send), (4, y_add), (5, y_done)] + gather + [(8, finish)]
 
     def b_unit(tick):
@@ -484,15 +485,15 @@
                                 fn(unit, unit % SLOTS)
 
     def compute_for(tick):
-        @pl.when(tick < UNITS_A)
-        def _():
-            compute_tile(tick)
+        @pl.when((tick < UNITS_A) & (tick % per_tile == 0))
+        def _():
+            compute_tile(tick // per_tile)
 
         fresh, unit = b_unit(tick)
 
-        @pl.when(fresh)
-        def _():
-            compute_tile(UNITS_A + unit)
+        @pl.when(fresh & (unit % per_tile == 0))
+        def _():
+            compute_tile((UNITS_A + unit) // per_tile)
 
     compute_for(0)
 
@@ -537,27 +538,30 @@
     gain_ref[...] = total
     pltpu.make_async_copy(gain_all.at[pl.ds(0, DATA - 1)], gain_all.at[pl.ds(0, DATA - 1)], gain_send).wait()
 
-    def backward_sent(mb, _):
-        @pl.when(pos > 0)
-        def _():
-            h_view = hout.at[rows_of(mb)]
-            pltpu.make_async_copy(h_view, h_view, send_sem.at[mb]).wait()
-
-        return 0
-
-    lax.fori_loop(0, n_mb, backward_sent, 0)
+    lax.fori_loop(0, SEQ_MB, functools.partial(sent, 1), 0)
+    lax.fori_loop(SEQ_MB, n_mb, functools.partial(sent, SEQ_MB), 0)
+
+    @pl.when(pos < last)
+    def _():
+        pltpu.make_async_copy(out_ref, out_ref, home_sem).wait()
+
+    for step in range(1, PIPE):
+        pltpu.make_async_copy(lens_buf.at[own_slab], lens_buf.at[own_slab], in_sem.at[step - 1]).wait()
     for src, _, send, _, target in spread:
-        place_done(src, send, target)
-
-
-def run_pass(acts, cots, lens_tile, w_qkv, w_out, w_up, w_down, gain_a, gain_m):
+        @pl.when(target != pos)
+        def _(src=src, send=send):
+            pltpu.make_async_copy(src, src, send).wait()
+
+
+def run_pass(acts, cots, lens, w_qkv, w_out, w_up, w_down, gain_a, gain_m):
     n_tok = acts.shape[0] * PIPE
-    n_mb = n_tok // ROWS
+    n_seq = n_tok // SEQ
+    n_mb = n_seq // SEQ_MB + SEQ_MB - 1
     any_spec = pl.BlockSpec(memory_space=pl.ANY)
     vmem_spec = pl.BlockSpec(memory_space=pltpu.VMEM)
     dma = pltpu.SemaphoreType.DMA
     return pl.pallas_call(
-        functools.partial(pass_kernel, n_mb),
+        functools.partial(pass_kernel, n_seq),
         out_shape=(
             jax.ShapeDtypeStruct(acts.shape, BF16),
             jax.ShapeDtypeStruct((D, 3 * D), F32),
@@ -566,14 +570,14 @@
             jax.ShapeDtypeStruct((FFN, D), F32),
             jax.ShapeDtypeStruct((8, D), F32),
         ),
-        in_specs=[any_spec] * 7 + [vmem_spec] * 2,
+        in_specs=[any_spec] * 2 + [pl.BlockSpec(memory_space=pltpu.SMEM)] + [any_spec] * 4 + [vmem_spec] * 2,
         out_specs=[any_spec] * 5 + [vmem_spec],
         scratch_shapes=[
             pltpu.VMEM((D, 3 * D), BF16),
             pltpu.VMEM((D, D), BF16),
             pltpu.VMEM((D, FFN), BF16),
             pltpu.VMEM((FFN, D), BF16),
-            pltpu.VMEM((n_mb * SEQ_MB, 8, 128), jnp.int32),
+            pltpu.VMEM((n_seq, 8, 128), jnp.int32),
             pltpu.VMEM((n_tok, D), BF16),
             pltpu.VMEM((n_tok, D), BF16),
             pltpu.VMEM((n_tok, D), BF16),
@@ -586,21 +590,21 @@
             pltpu.VMEM((n_tok * FFN // D, D), F32),
             pltpu.VMEM((n_tok, FFN), BF16),
             pltpu.VMEM((n_tok, D), BF16),
-            pltpu.VMEM((n_mb * UNIT, 128), F32),
-            pltpu.VMEM((UNIT, 128), F32),
+            pltpu.VMEM((n_tok * PAIRS, 128), F32),
+            pltpu.VMEM((SEQ_MB * PAIRS * SEQ, 128), F32),
             pltpu.VMEM((2, 8, D), F32),
             pltpu.VMEM((DATA, 8, D), F32),
         ] + [
             pltpu.VMEM((SLOTS, size, D), F32)
-            for size in (TILE // 2, TILE // 2, TILE // 2, TILE // LINE // 2, TILE, TILE) * 2
+            for size in (PART // 2, PART // 2, PART // 2, PART // LINE // 2, PART, PART) * 2
         ] + [
             dma((4,)),
-            dma((2 * (n_mb // PIPE) + PIPE,)),
+            dma((2 * (n_seq // PIPE) + PIPE - 1,)),
             dma((n_mb,)),
             dma((n_mb,)),
             dma((PIPE,)),
             dma((n_mb,)),
-            dma((n_mb // PIPE,)),
+            dma,
             dma((2, 6, SLOTS)),
             dma((3,)),
             dma((2, 3, SLOTS)),
@@ -609,7 +613,7 @@
             dma,
         ],
         compiler_params=pltpu.CompilerParams(collective_id=0, has_side_effects=True, vmem_limit_bytes=64 * 1024 * 1024 - 131072),
-    )(acts, cots, lens_tile, w_qkv, w_out, w_up, w_down, gain_a, gain_m)
+    )(acts, cots, lens, w_qkv, w_out, w_up, w_down, gain_a, gain_m)
 
 
 def solution(mesh):
@@ -617,10 +621,9 @@
     stage_spec = P('pipe')
 
     def device_pass(acts_in, cot_out, seq_lens, w_qkv, w_out, w_up, w_down, gain_attn, gain_mlp):
-        lens_tile = jnp.broadcast_to(seq_lens[:, None, None], (seq_lens.shape[0], 8, 128))
-        outs = run_pass(acts_in.reshape(-1, D), cot_out.reshape(-1, D), lens_tile, w_qkv.reshape(D, 3 * D),
+        outs = run_pass(acts_in.reshape(-1, D), cot_out.reshape(-1, D), seq_lens, w_qkv.reshape(D, 3 * D),
                         w_out.reshape(D, D), w_up.reshape(D, FFN), w_down.reshape(FFN, D),
-                        gain_attn.astype(F32), gain_mlp.astype(F32))
+                        gain_attn, gain_mlp)
         acts_out, g_qkv, g_out, g_up, g_down, g_gain = outs
         grads = (g_qkv.reshape(w_qkv.shape), g_out.reshape(w_out.shape), g_up.reshape(w_up.shape), g_down.reshape(w_down.shape),
                  g_gain[0:1], g_gain[1:2])

time: 348 us -> 348 us (level)
  Pallas kernels: 329 us -> 333 us
    pallas_call x1, Pallas kernels: 329 us -> 333 us  [run_pass(): pl.pallas_call(functools.partial(pass_kernel, n_seq), out_shape=(jax.Shap...]
where the time goes in v3:
time: 348 us
  Pallas kernels  333 us (96%)
  local copies, waits for them, and re-layouts  13.8 us (4%)
    pallas_call x1, Pallas kernels, run_pass(): pl.pallas_call(functools.partial(pass_kernel, n_seq), out_shape=(jax.Shap...  333 us
    unnamed x11, local copies, waits for them, and re-layouts  12.4 us

profile of v3, /device:TPU:0, one launch (start us, length us, event | category | flops | bytes accessed | tf_op | source)
XLA Modules:
  0.0 347.7 jit_solution(3241488233610970298)
XLA Ops:
  0.6 333.3 %shard_map.144 = (bf16[384,512]{1,0:T(8,128)(2,1)}, f32[512,1536]{1,0:T(8,128)}, f32[512,512]{1,0:T(8,128)}, f32[512,2048]{1,0:T(8,128)}, f32[2048,512]{1,0:T(8,128)}, /*index=5*/f32[8,512]{1,0:T(8,128)}) custom-call(bf16[384,512]{1,0:T(8,128)(2,1)} %bitcast.19, bf16[384,512]{1,0:T(8,128)(2,1)} %bitcast.20, s32[6]{0:T(128)} %lens_ref.1, ...), custom_call_target="tpu_custom_call" | custom-call | tf_op jit(solution)/shard_map/pallas_call | solution.py:563
  334.0 1.4 fusion
  335.3 1.8 copy.21
  337.1 0.0 copy-start.2
  337.1 0.0 copy-start.1
  337.1 3.9 %copy.22 = f32[1,512,1536]{2,1,0:T(8,128)} copy(f32[1,512,1536]{2,1,0:T(8,128)} %bitcast.13) | data formatting | bytes 6291456
  341.0 0.0 copy-done.2
  341.0 1.0 copy.23
  342.0 0.0 copy-done.1
  342.0 0.0 copy-start
  342.0 2.1 copy.24
  344.2 1.6 copy-done
  345.7 2.0 copy.25
Async XLA Ops:
  337.1 3.9 %copy-start.2 = (f32[512,512]{1,0:T(8,128)S(1)}, f32[512,512]{1,0:T(8,128)}, u32[]{:S(2)}) copy-start(f32[512,512]{1,0:T(8,128)} %get-tuple-element.15) | copy-start | bytes 3145732
  337.1 4.9 %copy-start.1 = (f32[512,2048]{1,0:T(8,128)S(1)}, f32[512,2048]{1,0:T(8,128)}, u32[]{:S(2)}) copy-start(f32[512,2048]{1,0:T(8,128)} %get-tuple-element.16) | copy-start | bytes 12582916
  342.0 3.7 %copy-start = (f32[2048,512]{1,0:T(8,128)S(1)}, f32[2048,512]{1,0:T(8,128)}, u32[]{:S(2)}) copy-start(f32[2048,512]{1,0:T(8,128)} %get-tuple-element.17) | copy-start | bytes 12582916
